TPU v7x, 512 devices: a whole 4x8x8 slice. The times are simulated.
512 devices in a mesh: row: 16 (over y_lo, z), col: 8 (over x, core), dp: 4 (over y_hi).
Axes of the slice: x: 4, y: 8 (y_hi: 4, y_lo: 2; y = y_hi * 2 + y_lo), z: 8, core: 2. Of those that a mesh axis runs over, the one named last changes fastest.
Arguments:
- tokens: bfloat16 [1536, 6144], P('dp', 'row'), parts along dimension 0, may hold values from -120 to 120
- norm_gain: float32 [6144], P('row'), may hold values from 0.25 to 1.75
- qkv_weight: bfloat16 [6144, 3, 3072], P('row', None, 'col'), may hold values from -2.5 to 2.5
- out_weight: bfloat16 [3072, 6144], P('col', 'row'), may hold values from -0.109375 to 0.109375
Outputs:
- projected: bfloat16 [1536, 6144], P('dp', 'row'), parts along dimension 0
There are 4 independent parts, one for each index of `dp`. A program takes and returns all parts, laid end to end along the dimension named above; an argument that names none is the same for every part. Nothing has to cross between parts.
All inputs are finite; a program needn't handle non-finite values.
Results may differ from a plain program's by a relative error of at most 0.025.
Values may be sent and summed in bfloat16 or wider, within the bound.
No kernel may reach another device: no remote copies, remote signals or barrier semaphores. Data moves between devices by JAX's collectives and lax.ppermute only.
A program may use at most 64 MiB of HBM per device.

v0:
```python
import math

import jax
import jax.numpy as jnp
from jax import lax
from jax.experimental import pallas as pl
from jax.experimental.pallas import tpu as pltpu
from jax.sharding import PartitionSpec as P

K = 128
EPSILON = 1e-05
EXTRA = 128
HALF = 64
LIMIT = pltpu.CompilerParams(vmem_limit_bytes=20 * 2**20)

CLASSES = 4
NEAR = [[8 * y + 2 * i + b for y in range(2) for b in range(2)] for i in range(4)]
FAR = [[8 * y + 2 * i + b for i in range(4)] for y in range(2) for b in range(2)]
CORES = [(c, c ^ 1) for c in range(8)]
CHIPS = [[0, 2, 4, 6], [1, 3, 5, 7]]


def rounded(a):
    return a.astype(jnp.bfloat16).astype(jnp.float32)


def dot32(a, b):
    return jnp.dot(a, b, preferred_element_type=jnp.float32)


def with_statistics(base, columns):
    lane = lax.broadcasted_iota(jnp.int32, base.shape, 1)
    middle, total, square = columns
    for at, column in enumerate(
        (middle, rounded(total), total - rounded(total), rounded(square), square - rounded(square))
    ):
        base = jnp.where(lane == at, column, base)
    return base.astype(jnp.bfloat16)


def statistics(extra):
    return extra[:, 0:1], extra[:, 1:2] + extra[:, 2:3], extra[:, 3:4] + extra[:, 4:5]


def partial_kernel(per, x_ref, g_ref, w_ref, o_ref):
    tokens, width = x_ref.shape
    columns = w_ref.shape[2]
    values = x_ref[...].astype(jnp.float32)
    middle = rounded(jnp.sum(values, axis=1, keepdims=True) / width)
    centered = values - middle
    total = jnp.sum(centered, axis=1, keepdims=True)
    square = jnp.sum(centered * centered, axis=1, keepdims=True)
    gain = g_ref[...].reshape(1, width)
    scaled = (centered * gain).astype(jnp.bfloat16)
    high = rounded(gain)
    line = lax.broadcasted_iota(jnp.int32, (16, width), 0)
    gains = jnp.where(line == 0, high, jnp.where(line == 1, gain - high, 0.0)).astype(jnp.bfloat16)
    row = lax.broadcasted_iota(jnp.int32, (per, EXTRA), 0)
    sums = jnp.zeros((per, EXTRA), jnp.float32)
    chunk = 0
    chunks = 3 * columns // EXTRA
    for part in range(3):
        weight = w_ref[part]
        o_ref[:, part * columns : (part + 1) * columns] = dot32(scaled, weight).astype(jnp.bfloat16)
        c = jnp.sum(dot32(gains, weight), axis=0, keepdims=True)
        for at in range(0, columns, EXTRA):
            piece = c[:, at : at + EXTRA]
            sums = jnp.where(row == chunk, piece, sums)
            sums = jnp.where(row == chunks + chunk, pltpu.roll(piece, HALF, 1), sums)
            chunk += 1
    base = jnp.concatenate([sums] * (tokens // per), axis=0)
    o_ref[:, 3 * columns :] = with_statistics(base, (middle, total, square))


def vector_sums(extras, chunks):
    upper = lax.broadcasted_iota(jnp.int32, (1, EXTRA), 1) >= HALF
    turned = [pltpu.roll(e, HALF, 1) for e in extras]
    return [
        [
            jnp.where(upper, e[at : at + 1], t[chunks + at : chunks + at + 1])
            for e, t in zip(extras, turned)
        ]
        for at in range(chunks)
    ]


def merge_kernel(per, width, r_ref, o_ref):
    terms = [r_ref.at[d] for d in range(r_ref.shape[0])]
    size = o_ref.shape[0]
    columns = o_ref.shape[1] - EXTRA
    chunks = columns // EXTRA
    extras = [t[:, columns:].astype(jnp.float32) for t in terms]
    held = [statistics(e) for e in extras]
    middle = rounded(sum(m + t / width for m, t, _ in held) / len(terms))
    shifts = [m - middle for m, _, _ in held]
    total = sum(t + width * s for s, (_, t, _) in zip(shifts, held))
    square = sum(q + 2.0 * s * t + width * (s * s) for s, (_, t, q) in zip(shifts, held))
    pieces = vector_sums([e[:per] for e in extras], chunks)
    wide = [jnp.broadcast_to(s, (size, EXTRA)) for s in shifts]
    for at in range(chunks):
        running = jnp.zeros((size, EXTRA), jnp.float32)
        for t, w, c in zip(terms, wide, pieces[at]):
            running = running + t[:, at * EXTRA : (at + 1) * EXTRA].astype(jnp.float32) + w * c
        o_ref[:, at * EXTRA : (at + 1) * EXTRA] = running.astype(jnp.bfloat16)
    lines = sum(e[:per] for e in extras)
    base = jnp.concatenate([lines] * (size // per), axis=0)
    o_ref[:, columns:] = with_statistics(base, (middle, total, square))


def norm_kernel(width, r_ref, o_ref):
    blocks, per, _ = r_ref.shape
    columns = o_ref.shape[1]
    chunks = columns // EXTRA
    extras = [r_ref[d, :, columns:].astype(jnp.float32) for d in range(blocks)]
    held = [statistics(e) for e in extras]
    average = sum(m + t / width for m, t, _ in held) / blocks
    shifts = [m - average for m, _, _ in held]
    variance = sum(
        q + 2.0 * s * t + width * (s * s) for s, (_, t, q) in zip(shifts, held)
    ) / (width * blocks)
    scale = lax.rsqrt(variance + EPSILON)
    wide = [jnp.broadcast_to(s, (per, EXTRA)) for s in shifts]
    pieces = vector_sums(extras, chunks)
    for at in range(chunks):
        running = jnp.zeros((per, EXTRA), jnp.float32)
        for d in range(blocks):
            term = r_ref[d, :, at * EXTRA : (at + 1) * EXTRA].astype(jnp.float32)
            running = running + term + wide[d] * pieces[at][d]
        o_ref[:, at * EXTRA : (at + 1) * EXTRA] = (running * scale).astype(jnp.bfloat16)


def attend_kernel(x_ref, w_ref, keep_ref, send_ref, whole_ref):
    columns = w_ref.shape[0]
    scaling = 1.0 / math.sqrt(K)
    outs = []
    for at in range(0, columns, K):
        q = x_ref[:, at : at + K]
        k = x_ref[:, columns + at : columns + at + K]
        v = x_ref[:, 2 * columns + at : 2 * columns + at + K]
        scores = (
            lax.dot_general(q, k, (((1,), (1,)), ((), ())), preferred_element_type=jnp.float32)
            * scaling
        )
        largest = jnp.max(scores, axis=1, keepdims=True)
        exponent = jnp.exp(scores - largest)
        inverse = 1.0 / jnp.sum(exponent, axis=1, keepdims=True)
        outs.append(dot32((exponent * inverse).astype(jnp.bfloat16), v).astype(jnp.bfloat16))
    whole_ref[...] = dot32(jnp.concatenate(outs, axis=1), w_ref[...]).astype(jnp.bfloat16)
    half = keep_ref.shape[0]
    core = lax.rem(lax.axis_index("col"), 2)
    keep_ref[...] = whole_ref[pl.ds(pl.multiple_of(core * half, half), half), :]
    send_ref[...] = whole_ref[pl.ds(pl.multiple_of((1 - core) * half, half), half), :]


def exchange(a, axis, groups):
    return lax.all_to_all(a, axis, 0, 0, tiled=True, axis_index_groups=groups)


def spread(a, axis, groups):
    return exchange(jnp.broadcast_to(a[None], (len(groups[0]), *a.shape)), axis, groups)


def like(shape):
    return jax.ShapeDtypeStruct(shape, jnp.bfloat16)


def shards(tokens, norm_gain, qkv_weight, out_weight):
    count, width = tokens.shape
    columns = qkv_weight.shape[2]
    size = count // CLASSES
    per = size // len(FAR[0])
    wide = 3 * columns + EXTRA
    payload = pl.pallas_call(
        lambda *refs: partial_kernel(per, *refs),
        out_shape=like((count, wide)),
        name="partial",
        compiler_params=LIMIT,
    )(tokens, norm_gain, jnp.transpose(qkv_weight, (1, 0, 2)))
    near = exchange(payload.reshape(CLASSES, size, wide), "row", NEAR)
    merged = pl.pallas_call(
        lambda *refs: merge_kernel(per, width, *refs),
        out_shape=like((size, wide)),
        name="merge",
        compiler_params=LIMIT,
    )(near)
    far = exchange(merged.reshape(-1, per, wide), "row", FAR)
    mine = pl.pallas_call(
        lambda *refs: norm_kernel(width * CLASSES, *refs),
        out_shape=like((per, 3 * columns)),
        name="norm",
        compiler_params=LIMIT,
    )(far)
    block = spread(mine, "row", FAR).reshape(size, 3 * columns)
    qkv = spread(block, "row", NEAR).reshape(count, 3 * columns)
    keep, send = pl.pallas_call(
        attend_kernel,
        out_shape=[like((count // 2, width))] * 2,
        scratch_shapes=[pltpu.VMEM((count, width), jnp.bfloat16)],
        name="attend",
        compiler_params=LIMIT,
    )(qkv, out_weight)
    other = lax.ppermute(send, "col", CORES)
    pair = (keep.astype(jnp.float32) + other.astype(jnp.float32)).astype(jnp.bfloat16)
    terms = spread(pair, "col", CHIPS)
    half = jnp.sum(terms.astype(jnp.float32), axis=0).astype(jnp.bfloat16)
    rest = lax.ppermute(half, "col", CORES)
    core = lax.rem(lax.axis_index("col"), 2)
    return jnp.concatenate(
        [jnp.where(core == 0, half, rest), jnp.where(core == 0, rest, half)], axis=0
    )


def solution(mesh):
    in_specs = (P("dp", "row"), P("row"), P("row", None, "col"), P("col", "row"))
    out_specs = P("dp", "row")
    return jax.shard_map(shards, mesh=mesh, in_specs=in_specs, out_specs=out_specs, check_vma=False)
```

profile of v0, /device:TPU:1, one launch (start us, length us, event | category | flops | bytes accessed | tf_op | source)
XLA Modules:
  0.0 91.0 jit_solution(1194761826288579258)
XLA Ops:
  0.0 0.0 copy-start
  0.0 1.2 %copy-done = bf16[384,3,384]{2,0,1:T(8,128)(2,1)S(1)} copy-done((bf16[384,3,384]{2,0,1:T(8,128)(2,1)S(1)}, bf16[384,3,384]{2,0,1:T(8,128)(2,1)}, u32[]{:S(2)}) %copy-start) | copy-done | bytes 884760
  1.2 0.0 copy-start.1
  1.2 1.0 %copy-done.1 = bf16[384,384]{1,0:T(8,128)(2,1)S(1)} copy-done((bf16[384,384]{1,0:T(8,128)(2,1)S(1)}, bf16[384,384]{1,0:T(8,128)(2,1)}, u32[]{:S(2)}) %copy-start.1) | copy-done | bytes 294936
  2.1 0.0 copy-start.3
  2.1 0.7 copy-done.3
  2.8 1.0 %partial.1 = bf16[384,1280]{1,0:T(8,128)(2,1)S(1)} custom-call(bf16[384,384]{1,0:T(8,128)(2,1)S(1)} %copy-done.1, f32[384]{0:T(512)S(1)} %copy-done.3, bf16[3,384,384]{2,1,0:T(8,128)(2,1)S(1)} %bitcast.8), custom_call_target="tpu_custom_call" | custom-call | tf_op jit(solution)/shard_map/partial/pallas_call | solution.py:173
  3.9 14.2 %all_to_all.25.refs_0_ = bf16[4,96,1280]{2,1,0:T(8,128)(2,1)S(1)} all-to-all(bf16[4,96,1280]{2,1,0:T(8,128)(2,1)S(1)} %bitcast.5), channel_id=1, replica_groups={{0,32,256,288},{64,96,320,352},{128,160,384,416},{192,224,448,480},{1,3..., dimensions={0} | all-to-all | bytes 1966080 | tf_op jit(solution)/shard_map/all_to_all | solution.py:156
  18.1 0.9 merge.1
  19.0 20.7 %all_to_all.26.refs_0_ = bf16[4,24,1280]{2,1,0:T(8,128)(2,1)S(1)} all-to-all(bf16[4,24,1280]{2,1,0:T(8,128)(2,1)S(1)} %bitcast.7), channel_id=1, replica_groups={{0,64,128,192},{32,96,160,224},{256,320,384,448},{288,352,416,480},{1,6..., dimensions={0} | all-to-all | bytes 491520 | tf_op jit(solution)/shard_map/all_to_all | solution.py:156
  39.6 0.3 norm.1
  40.0 10.5 %all_to_all.27 = bf16[4,24,1152]{2,1,0:T(8,128)(2,1)S(1)} all-to-all(bf16[4,24,1152]{2,1,0:T(8,128)(2,1)S(1)} %broadcast_in_dim.8), channel_id=1, replica_groups={{0,64,128,192},{32,96,160,224},{256,320,384,448},{288,352,416,480},{1,6..., dimensions={0} | all-to-all | bytes 442368 | tf_op jit(solution)/shard_map/all_to_all | solution.py:156
  50.5 0.1 broadcast_in_dim.10
  50.6 0.0 copy-start.2
  50.6 10.8 %all_to_all.28 = bf16[4,96,1152]{2,1,0:T(8,128)(2,1)S(1)} all-to-all(bf16[4,96,1152]{2,1,0:T(8,128)(2,1)S(1)} %broadcast_in_dim.10), channel_id=1, replica_groups={{0,32,256,288},{64,96,320,352},{128,160,384,416},{192,224,448,480},{1,3..., dimensions={0} | all-to-all | bytes 1769472 | tf_op jit(solution)/shard_map/all_to_all | solution.py:156
  61.4 0.0 copy-done.2
  61.4 1.7 %attend.1 = (bf16[192,384]{1,0:T(8,128)(2,1)S(1)}, bf16[192,384]{1,0:T(8,128)(2,1)S(1)}) custom-call(bf16[384,1152]{1,0:T(8,128)(2,1)S(1)} %bitcast.6, bf16[384,384]{1,0:T(8,128)(2,1)S(1)} %copy-done.2), custom_call_target="tpu_custom_call" | custom-call | tf_op jit(solution)/shard_map/attend/pallas_call | solution.py:195
  63.1 8.0 %collective-permute-start = (bf16[192,384]{1,0:T(8,128)(2,1)S(1)}, bf16[192,384]{1,0:T(8,128)(2,1)S(1)}, u32[]{:S(2)}, u32[]{:S(2)}) collective-permute-start(bf16[192,384]{1,0:T(8,128)(2,1)S(1)} %get-tuple-element.8), channel_id=1, source_target_pairs={{0,4},{4,0},{8,12},{12,8},{16,20},{20,16},{24,28},{28,24},{1,5},{5... | collective-permute-start | bytes 442376 | tf_op jit(solution)/shard_map/ppermute | solution.py:202
  71.1 1.0 %collective-permute-done = bf16[192,384]{1,0:T(8,128)(2,1)S(1)} collective-permute-done((bf16[192,384]{1,0:T(8,128)(2,1)S(1)}, bf16[192,384]{1,0:T(8,128)(2,1)S(1)}, u32[]{:S(2)}, u32[]{:S(2)}) %collective-permute-start) | collective-permute-done | bytes 147488 | tf_op jit(solution)/shard_map/ppermute | solution.py:202
  72.2 0.1 broadcast_in_dim.22
  72.2 13.5 %all_to_all.29 = bf16[4,192,384]{2,1,0:T(8,128)(2,1)S(1)} all-to-all(bf16[4,192,384]{2,1,0:T(8,128)(2,1)S(1)} %broadcast_in_dim.22), channel_id=1, replica_groups={{0,8,16,24},{4,12,20,28},{1,9,17,25},{5,13,21,29},{2,10,18,26},{6,14,22..., dimensions={0} | all-to-all | bytes 1179648 | tf_op jit(solution)/shard_map/all_to_all | solution.py:156
  85.7 0.1 reduce_sum.12
  85.8 3.4 %collective-permute-start.1 = (bf16[192,384]{1,0:T(8,128)(2,1)S(1)}, bf16[192,384]{1,0:T(8,128)(2,1)S(1)}, u32[]{:S(2)}, u32[]{:S(2)}) collective-permute-start(bf16[192,384]{1,0:T(8,128)(2,1)S(1)} %reduce_sum.12), channel_id=1, source_target_pairs={{0,4},{4,0},{8,12},{12,8},{16,20},{20,16},{24,28},{28,24},{1,5},{5... | collective-permute-start | bytes 442376 | tf_op jit(solution)/shard_map/ppermute | solution.py:206
  89.2 1.0 %collective-permute-done.1 = bf16[192,384]{1,0:T(8,128)(2,1)S(1)} collective-permute-done((bf16[192,384]{1,0:T(8,128)(2,1)S(1)}, bf16[192,384]{1,0:T(8,128)(2,1)S(1)}, u32[]{:S(2)}, u32[]{:S(2)}) %collective-permute-start.1) | collective-permute-done | bytes 147488 | tf_op jit(solution)/shard_map/ppermute | solution.py:206
  90.2 0.7 pad_maximum_fusion
  (3 shorter events, 0.1 us)
Async XLA Ops:
  0.0 1.2 %copy-start = (bf16[384,3,384]{2,0,1:T(8,128)(2,1)S(1)}, bf16[384,3,384]{2,0,1:T(8,128)(2,1)}, u32[]{:S(2)}) copy-start(bf16[384,3,384]{2,0,1:T(8,128)(2,1)} %param.6) | copy-start | bytes 2654212
  1.2 1.0 %copy-start.1 = (bf16[384,384]{1,0:T(8,128)(2,1)S(1)}, bf16[384,384]{1,0:T(8,128)(2,1)}, u32[]{:S(2)}) copy-start(bf16[384,384]{1,0:T(8,128)(2,1)} %refs_0_.1) | copy-start | bytes 884740
  2.1 0.7 copy-start.3
  50.6 10.8 %copy-start.2 = (bf16[384,384]{1,0:T(8,128)(2,1)S(1)}, bf16[384,384]{1,0:T(8,128)(2,1)}, u32[]{:S(2)}) copy-start(bf16[384,384]{1,0:T(8,128)(2,1)} %w_ref.1) | copy-start | bytes 884740
  63.1 9.0 %collective-permute-start = (bf16[192,384]{1,0:T(8,128)(2,1)S(1)}, bf16[192,384]{1,0:T(8,128)(2,1)S(1)}, u32[]{:S(2)}, u32[]{:S(2)}) collective-permute-start(bf16[192,384]{1,0:T(8,128)(2,1)S(1)} %get-tuple-element.8), channel_id=1, source_target_pairs={{0,4},{4,0},{8,12},{12,8},{16,20},{20,16},{24,28},{28,24},{1,5},{5... | collective-permute-start | bytes 442376 | tf_op jit(solution)/shard_map/ppermute | solution.py:202
  85.8 4.4 %collective-permute-start.1 = (bf16[192,384]{1,0:T(8,128)(2,1)S(1)}, bf16[192,384]{1,0:T(8,128)(2,1)S(1)}, u32[]{:S(2)}, u32[]{:S(2)}) collective-permute-start(bf16[192,384]{1,0:T(8,128)(2,1)S(1)} %reduce_sum.12), channel_id=1, source_target_pairs={{0,4},{4,0},{8,12},{12,8},{16,20},{20,16},{24,28},{28,24},{1,5},{5... | collective-permute-start | bytes 442376 | tf_op jit(solution)/shard_map/ppermute | solution.py:206
where the time goes:
time: 91.4 us; the launch traced here: 91 us
  blocking collectives  69.7 us (76%)
  starting transfers between devices  11.4 us (12%)
  Pallas kernels  3.97 us (4%)
  local copies, waits for them, and re-layouts  2.95 us (3%)
  waiting for transfers between devices  1.96 us (2%)
    all_to_all x5, blocking collectives, exchange(): return lax.all_to_all(a, axis, 0, 0, tiled=True, axis_index_groups=groups)  69.7 us
    ppermute x1, starting transfers between devices, shards(): other = lax.ppermute(send, 'col', CORES)  8.01 us
    ppermute x1, starting transfers between devices, shards(): rest = lax.ppermute(half, 'col', CORES)  3.41 us
    unnamed x8, local copies, waits for them, and re-layouts  2.82 us
  transfers between devices with their start and end apart: 2, of which 2 were waited for; matrix products, arithmetic and copies ran while one was open for 0% of the time, Pallas kernels for 0%

commit v1 on v0

--- a/solution.py
+++ b/solution.py
@@ -11,13 +11,15 @@
 EPSILON = 1e-05
 EXTRA = 128
 HALF = 64
+FIRST = pltpu.CompilerParams(vmem_limit_bytes=20 * 2**20)
 LIMIT = pltpu.CompilerParams(vmem_limit_bytes=20 * 2**20)
 
 CLASSES = 4
 NEAR = [[8 * y + 2 * i + b for y in range(2) for b in range(2)] for i in range(4)]
 FAR = [[8 * y + 2 * i + b for i in range(4)] for y in range(2) for b in range(2)]
 CORES = [(c, c ^ 1) for c in range(8)]
-CHIPS = [[0, 2, 4, 6], [1, 3, 5, 7]]
+RIGHT = [(c, c ^ 2) for c in range(8)]
+LEFT = [(c, (c - 2 if c & 2 == 0 else c + 2) % 8) for c in range(8)]
 
 
 def rounded(a):
@@ -129,12 +131,16 @@
         o_ref[:, at * EXTRA : (at + 1) * EXTRA] = (running * scale).astype(jnp.bfloat16)
 
 
-def attend_kernel(x_ref, w_ref, keep_ref, send_ref, whole_ref):
+def attend_kernel(other, x_ref, w_ref, o_ref):
     columns = w_ref.shape[0]
+    half = o_ref.shape[0]
+    core = lax.rem(lax.axis_index("col"), 2)
+    which = 1 - core if other else core
+    lines = pl.ds(pl.multiple_of(which * half, half), half)
     scaling = 1.0 / math.sqrt(K)
     outs = []
     for at in range(0, columns, K):
-        q = x_ref[:, at : at + K]
+        q = x_ref[lines, at : at + K]
         k = x_ref[:, columns + at : columns + at + K]
         v = x_ref[:, 2 * columns + at : 2 * columns + at + K]
         scores = (
@@ -145,11 +151,26 @@
         exponent = jnp.exp(scores - largest)
         inverse = 1.0 / jnp.sum(exponent, axis=1, keepdims=True)
         outs.append(dot32((exponent * inverse).astype(jnp.bfloat16), v).astype(jnp.bfloat16))
-    whole_ref[...] = dot32(jnp.concatenate(outs, axis=1), w_ref[...]).astype(jnp.bfloat16)
-    half = keep_ref.shape[0]
-    core = lax.rem(lax.axis_index("col"), 2)
-    keep_ref[...] = whole_ref[pl.ds(pl.multiple_of(core * half, half), half), :]
-    send_ref[...] = whole_ref[pl.ds(pl.multiple_of((1 - core) * half, half), half), :]
+    o_ref[...] = dot32(jnp.concatenate(outs, axis=1), w_ref[...]).astype(jnp.bfloat16)
+
+
+def attend(other, qkv, weight):
+    count, wide = qkv.shape
+    width = weight.shape[1]
+    flops = 2 * (count // 2) * (2 * count * weight.shape[0] + weight.shape[0] * width)
+    return pl.pallas_call(
+        lambda *refs: attend_kernel(other, *refs),
+        out_shape=like((count // 2, width)),
+        name="attend",
+        compiler_params=LIMIT,
+        cost_estimate=pl.CostEstimate(
+            flops=4 * flops, bytes_accessed=2 * count * wide, transcendentals=0
+        ),
+    )(qkv, weight)
+
+
+def added(a, b):
+    return (a.astype(jnp.float32) + b.astype(jnp.float32)).astype(jnp.bfloat16)
 
 
 def exchange(a, axis, groups):
@@ -174,7 +195,7 @@
         lambda *refs: partial_kernel(per, *refs),
         out_shape=like((count, wide)),
         name="partial",
-        compiler_params=LIMIT,
+        compiler_params=FIRST,
     )(tokens, norm_gain, jnp.transpose(qkv_weight, (1, 0, 2)))
     near = exchange(payload.reshape(CLASSES, size, wide), "row", NEAR)
     merged = pl.pallas_call(
@@ -192,17 +213,10 @@
     )(far)
     block = spread(mine, "row", FAR).reshape(size, 3 * columns)
     qkv = spread(block, "row", NEAR).reshape(count, 3 * columns)
-    keep, send = pl.pallas_call(
-        attend_kernel,
-        out_shape=[like((count // 2, width))] * 2,
-        scratch_shapes=[pltpu.VMEM((count, width), jnp.bfloat16)],
-        name="attend",
-        compiler_params=LIMIT,
-    )(qkv, out_weight)
-    other = lax.ppermute(send, "col", CORES)
-    pair = (keep.astype(jnp.float32) + other.astype(jnp.float32)).astype(jnp.bfloat16)
-    terms = spread(pair, "col", CHIPS)
-    half = jnp.sum(terms.astype(jnp.float32), axis=0).astype(jnp.bfloat16)
+    send = lax.ppermute(attend(True, qkv, out_weight), "col", CORES)
+    pair = added(attend(False, qkv, out_weight), send)
+    four = added(pair, lax.ppermute(pair, "col", RIGHT))
+    half = added(four, lax.ppermute(four, "col", LEFT))
     rest = lax.ppermute(half, "col", CORES)
     core = lax.rem(lax.axis_index("col"), 2)
     return jnp.concatenate(

time: 91.4 us -> 93.2 us (1.020)
  blocking collectives: 69.7 us -> 56.2 us
  starting transfers between devices: 11.4 us -> 19.2 us
  waiting for transfers between devices: 1.96 us -> 8.38 us
  Pallas kernels: 3.97 us -> 5.04 us
    all_to_all x5 -> x4, blocking collectives: 69.7 us -> 56.2 us  [exchange(): return lax.all_to_all(a, axis, 0, 0, tiled=True, axis_index_groups=groups)]
    ppermute x1 -> x3, starting transfers between devices: 8.01 us -> 15.5 us  [the longest x1 8.02 us: shards(): send = lax.ppermute(attend(True, qkv, out_weight), 'col', CORES)]
    ppermute x1 -> x3, waiting for transfers between devices: 0.99 us -> 7.4 us  [the longest x1 4.15 us: shards(): four = added(pair, lax.ppermute(pair, 'col', RIGHT))]
    pallas_call x1 -> x2, Pallas kernels: 1.72 us -> 2.78 us  [attend(): pl.pallas_call(lambda *refs: attend_kernel(other, *refs), out_shape=like(...]
  transfers between devices with their start and end apart: 2 -> 4, of which waited for: 2 -> 3; matrix products, arithmetic and copies ran while one was open for 0% -> 0% of each run, Pallas kernels for 0% -> 2%
where the time goes in v1:
time: 93.2 us; the launch traced here: 92.7 us
  blocking collectives  56.2 us (60%)
  starting transfers between devices  19.2 us (21%)
  waiting for transfers between devices  8.38 us (9%)
  Pallas kernels  5.04 us (5%)
  local copies, waits for them, and re-layouts  2.9 us (3%)
    all_to_all x4, blocking collectives, exchange(): return lax.all_to_all(a, axis, 0, 0, tiled=True, axis_index_groups=groups)  56.2 us
    ppermute x1, starting transfers between devices, shards(): send = lax.ppermute(attend(True, qkv, out_weight), 'col', CORES)  8.02 us
    ppermute x1, starting transfers between devices, shards(): half = added(four, lax.ppermute(four, 'col', LEFT))  4.39 us
    ppermute x1, waiting for transfers between devices, shards(): four = added(pair, lax.ppermute(pair, 'col', RIGHT))  4.15 us
    ppermute x1, starting transfers between devices, shards(): rest = lax.ppermute(half, 'col', CORES)  3.63 us
    ppermute x1, waiting for transfers between devices, shards(): half = added(four, lax.ppermute(four, 'col', LEFT))  3.25 us
    ppermute x1, starting transfers between devices, shards(): four = added(pair, lax.ppermute(pair, 'col', RIGHT))  3.13 us
    unnamed x8, local copies, waits for them, and re-layouts  2.82 us
  transfers between devices with their start and end apart: 4, of which 3 were waited for; matrix products, arithmetic and copies ran while one was open for 0% of the time, Pallas kernels for 2%

profile of v1, /device:TPU:1, one launch (start us, length us, event | category | flops | bytes accessed | tf_op | source)
XLA Modules:
  0.0 92.7 jit_solution(10076795391254847619)
XLA Ops:
  0.0 0.0 copy-start
  0.0 1.2 %copy-done = bf16[384,3,384]{2,0,1:T(8,128)(2,1)S(1)} copy-done((bf16[384,3,384]{2,0,1:T(8,128)(2,1)S(1)}, bf16[384,3,384]{2,0,1:T(8,128)(2,1)}, u32[]{:S(2)}) %copy-start) | copy-done | bytes 884760
  1.2 0.0 copy-start.1
  1.2 1.0 %copy-done.1 = bf16[384,384]{1,0:T(8,128)(2,1)S(1)} copy-done((bf16[384,384]{1,0:T(8,128)(2,1)S(1)}, bf16[384,384]{1,0:T(8,128)(2,1)}, u32[]{:S(2)}) %copy-start.1) | copy-done | bytes 294936
  2.1 0.0 copy-start.2
  2.1 0.7 copy-done.2
  2.8 1.0 %partial.1 = bf16[384,1280]{1,0:T(8,128)(2,1)S(1)} custom-call(bf16[384,384]{1,0:T(8,128)(2,1)S(1)} %copy-done.1, f32[384]{0:T(512)S(1)} %copy-done.2, bf16[3,384,384]{2,1,0:T(8,128)(2,1)S(1)} %bitcast.7), custom_call_target="tpu_custom_call" | custom-call | tf_op jit(solution)/shard_map/partial/pallas_call | solution.py:194
  3.9 14.2 %all_to_all.20.refs_0_ = bf16[4,96,1280]{2,1,0:T(8,128)(2,1)S(1)} all-to-all(bf16[4,96,1280]{2,1,0:T(8,128)(2,1)S(1)} %bitcast.5), channel_id=1, replica_groups={{0,32,256,288},{64,96,320,352},{128,160,384,416},{192,224,448,480},{1,3..., dimensions={0} | all-to-all | bytes 1966080 | tf_op jit(solution)/shard_map/all_to_all | solution.py:177
  18.1 0.9 merge.1
  19.0 20.7 %all_to_all.21.refs_0_ = bf16[4,24,1280]{2,1,0:T(8,128)(2,1)S(1)} all-to-all(bf16[4,24,1280]{2,1,0:T(8,128)(2,1)S(1)} %bitcast.6), channel_id=1, replica_groups={{0,64,128,192},{32,96,160,224},{256,320,384,448},{288,352,416,480},{1,6..., dimensions={0} | all-to-all | bytes 491520 | tf_op jit(solution)/shard_map/all_to_all | solution.py:177
  39.6 0.3 norm.1
  40.0 10.5 %all_to_all.22 = bf16[4,24,1152]{2,1,0:T(8,128)(2,1)S(1)} all-to-all(bf16[4,24,1152]{2,1,0:T(8,128)(2,1)S(1)} %broadcast_in_dim.6), channel_id=1, replica_groups={{0,64,128,192},{32,96,160,224},{256,320,384,448},{288,352,416,480},{1,6..., dimensions={0} | all-to-all | bytes 442368 | tf_op jit(solution)/shard_map/all_to_all | solution.py:177
  50.5 0.1 broadcast_in_dim.15
  50.6 0.0 copy-start.3
  50.6 10.8 %all_to_all.23 = bf16[4,96,1152]{2,1,0:T(8,128)(2,1)S(1)} all-to-all(bf16[4,96,1152]{2,1,0:T(8,128)(2,1)S(1)} %broadcast_in_dim.15), channel_id=1, replica_groups={{0,32,256,288},{64,96,320,352},{128,160,384,416},{192,224,448,480},{1,3..., dimensions={0} | all-to-all | bytes 1769472 | tf_op jit(solution)/shard_map/all_to_all | solution.py:177
  61.4 0.0 copy-done.3
  61.4 1.4 %attend.3 = bf16[192,384]{1,0:T(8,128)(2,1)S(1)} custom-call(bf16[384,1152]{1,0:T(8,128)(2,1)S(1)} %bitcast.8, bf16[384,384]{1,0:T(8,128)(2,1)S(1)} %copy-done.3), custom_call_target="tpu_custom_call" | custom-call | flops 679477248 | bytes 884736 | tf_op jit(solution)/shard_map/attend/pallas_call | solution.py:161
  62.8 8.0 %collective-permute-start = (bf16[192,384]{1,0:T(8,128)(2,1)S(1)}, bf16[192,384]{1,0:T(8,128)(2,1)S(1)}, u32[]{:S(2)}, u32[]{:S(2)}) collective-permute-start(bf16[192,384]{1,0:T(8,128)(2,1)S(1)} %attend.3), channel_id=1, source_target_pairs={{0,4},{4,0},{8,12},{12,8},{16,20},{20,16},{24,28},{28,24},{1,5},{5... | collective-permute-start | bytes 442376 | tf_op jit(solution)/shard_map/ppermute | solution.py:216
  70.8 1.4 %attend.2 = bf16[192,384]{1,0:T(8,128)(2,1)S(1)} custom-call(bf16[384,1152]{1,0:T(8,128)(2,1)S(1)} %bitcast.9, bf16[384,384]{1,0:T(8,128)(2,1)S(1)} %copy-done.3), custom_call_target="tpu_custom_call" | custom-call | flops 679477248 | bytes 884736 | tf_op jit(solution)/shard_map/attend/pallas_call | solution.py:161
  72.2 0.0 collective-permute-done
  72.3 3.1 %collective-permute-start.1 = (bf16[192,384]{1,0:T(8,128)(2,1)S(1)}, bf16[192,384]{1,0:T(8,128)(2,1)S(1)}, u32[]{:S(2)}, u32[]{:S(2)}) collective-permute-start(bf16[192,384]{1,0:T(8,128)(2,1)S(1)} %add_convert_fusion.2), channel_id=1, source_target_pairs={{0,8},{4,12},{8,0},{12,4},{16,24},{20,28},{24,16},{28,20},{1,9},{5... | collective-permute-start | bytes 442376 | tf_op jit(solution)/shard_map/ppermute | solution.py:218
  75.4 4.1 %collective-permute-done.1 = bf16[192,384]{1,0:T(8,128)(2,1)S(1)} collective-permute-done((bf16[192,384]{1,0:T(8,128)(2,1)S(1)}, bf16[192,384]{1,0:T(8,128)(2,1)S(1)}, u32[]{:S(2)}, u32[]{:S(2)}) %collective-permute-start.1) | collective-permute-done | bytes 147488 | tf_op jit(solution)/shard_map/ppermute | solution.py:218
  79.6 4.4 %collective-permute-start.2 = (bf16[192,384]{1,0:T(8,128)(2,1)S(1)}, bf16[192,384]{1,0:T(8,128)(2,1)S(1)}, u32[]{:S(2)}, u32[]{:S(2)}) collective-permute-start(bf16[192,384]{1,0:T(8,128)(2,1)S(1)} %add_convert_fusion.1), channel_id=1, source_target_pairs={{0,24},{4,28},{8,16},{12,20},{16,8},{20,12},{24,0},{28,4},{1,25},{... | collective-permute-start | bytes 442376 | tf_op jit(solution)/shard_map/ppermute | solution.py:219
  84.0 3.2 %collective-permute-done.2 = bf16[192,384]{1,0:T(8,128)(2,1)S(1)} collective-permute-done((bf16[192,384]{1,0:T(8,128)(2,1)S(1)}, bf16[192,384]{1,0:T(8,128)(2,1)S(1)}, u32[]{:S(2)}, u32[]{:S(2)}) %collective-permute-start.2) | collective-permute-done | bytes 147488 | tf_op jit(solution)/shard_map/ppermute | solution.py:219
  87.3 3.6 %collective-permute-start.3 = (bf16[192,384]{1,0:T(8,128)(2,1)S(1)}, bf16[192,384]{1,0:T(8,128)(2,1)S(1)}, u32[]{:S(2)}, u32[]{:S(2)}) collective-permute-start(bf16[192,384]{1,0:T(8,128)(2,1)S(1)} %add_convert_fusion), channel_id=1, source_target_pairs={{0,4},{4,0},{8,12},{12,8},{16,20},{20,16},{24,28},{28,24},{1,5},{5... | collective-permute-start | bytes 442376 | tf_op jit(solution)/shard_map/ppermute | solution.py:220
  91.0 1.0 %collective-permute-done.3 = bf16[192,384]{1,0:T(8,128)(2,1)S(1)} collective-permute-done((bf16[192,384]{1,0:T(8,128)(2,1)S(1)}, bf16[192,384]{1,0:T(8,128)(2,1)S(1)}, u32[]{:S(2)}, u32[]{:S(2)}) %collective-permute-start.3) | collective-permute-done | bytes 147488 | tf_op jit(solution)/shard_map/ppermute | solution.py:220
  92.0 0.7 pad_maximum_fusion
  (5 shorter events, 0.2 us)
Async XLA Ops:
  0.0 1.2 %copy-start = (bf16[384,3,384]{2,0,1:T(8,128)(2,1)S(1)}, bf16[384,3,384]{2,0,1:T(8,128)(2,1)}, u32[]{:S(2)}) copy-start(bf16[384,3,384]{2,0,1:T(8,128)(2,1)} %param.6) | copy-start | bytes 2654212
  1.2 1.0 %copy-start.1 = (bf16[384,384]{1,0:T(8,128)(2,1)S(1)}, bf16[384,384]{1,0:T(8,128)(2,1)}, u32[]{:S(2)}) copy-start(bf16[384,384]{1,0:T(8,128)(2,1)} %refs_0_.1) | copy-start | bytes 884740
  2.1 0.7 copy-start.2
  50.6 10.8 %copy-start.3 = (bf16[384,384]{1,0:T(8,128)(2,1)S(1)}, bf16[384,384]{1,0:T(8,128)(2,1)}, u32[]{:S(2)}) copy-start(bf16[384,384]{1,0:T(8,128)(2,1)} %refs_1_.5) | copy-start | bytes 884740
  62.8 9.4 %collective-permute-start = (bf16[192,384]{1,0:T(8,128)(2,1)S(1)}, bf16[192,384]{1,0:T(8,128)(2,1)S(1)}, u32[]{:S(2)}, u32[]{:S(2)}) collective-permute-start(bf16[192,384]{1,0:T(8,128)(2,1)S(1)} %attend.3), channel_id=1, source_target_pairs={{0,4},{4,0},{8,12},{12,8},{16,20},{20,16},{24,28},{28,24},{1,5},{5... | collective-permute-start | bytes 442376 | tf_op jit(solution)/shard_map/ppermute | solution.py:216
  72.3 7.3 %collective-permute-start.1 = (bf16[192,384]{1,0:T(8,128)(2,1)S(1)}, bf16[192,384]{1,0:T(8,128)(2,1)S(1)}, u32[]{:S(2)}, u32[]{:S(2)}) collective-permute-start(bf16[192,384]{1,0:T(8,128)(2,1)S(1)} %add_convert_fusion.2), channel_id=1, source_target_pairs={{0,8},{4,12},{8,0},{12,4},{16,24},{20,28},{24,16},{28,20},{1,9},{5... | collective-permute-start | bytes 442376 | tf_op jit(solution)/shard_map/ppermute | solution.py:218
  79.6 7.6 %collective-permute-start.2 = (bf16[192,384]{1,0:T(8,128)(2,1)S(1)}, bf16[192,384]{1,0:T(8,128)(2,1)S(1)}, u32[]{:S(2)}, u32[]{:S(2)}) collective-permute-start(bf16[192,384]{1,0:T(8,128)(2,1)S(1)} %add_convert_fusion.1), channel_id=1, source_target_pairs={{0,24},{4,28},{8,16},{12,20},{16,8},{20,12},{24,0},{28,4},{1,25},{... | collective-permute-start | bytes 442376 | tf_op jit(solution)/shard_map/ppermute | solution.py:219
  87.3 4.6 %collective-permute-start.3 = (bf16[192,384]{1,0:T(8,128)(2,1)S(1)}, bf16[192,384]{1,0:T(8,128)(2,1)S(1)}, u32[]{:S(2)}, u32[]{:S(2)}) collective-permute-start(bf16[192,384]{1,0:T(8,128)(2,1)S(1)} %add_convert_fusion), channel_id=1, source_target_pairs={{0,4},{4,0},{8,12},{12,8},{16,20},{20,16},{24,28},{28,24},{1,5},{5... | collective-permute-start | bytes 442376 | tf_op jit(solution)/shard_map/ppermute | solution.py:220

commit v2 on v1

--- a/solution.py
+++ b/solution.py
@@ -11,15 +11,13 @@
 EPSILON = 1e-05
 EXTRA = 128
 HALF = 64
-FIRST = pltpu.CompilerParams(vmem_limit_bytes=20 * 2**20)
 LIMIT = pltpu.CompilerParams(vmem_limit_bytes=20 * 2**20)
 
 CLASSES = 4
 NEAR = [[8 * y + 2 * i + b for y in range(2) for b in range(2)] for i in range(4)]
 FAR = [[8 * y + 2 * i + b for i in range(4)] for y in range(2) for b in range(2)]
 CORES = [(c, c ^ 1) for c in range(8)]
-RIGHT = [(c, c ^ 2) for c in range(8)]
-LEFT = [(c, (c - 2 if c & 2 == 0 else c + 2) % 8) for c in range(8)]
+CHIPS = [[0, 2, 4, 6], [1, 3, 5, 7]]
 
 
 def rounded(a):
@@ -44,16 +42,22 @@
     return extra[:, 0:1], extra[:, 1:2] + extra[:, 2:3], extra[:, 3:4] + extra[:, 4:5]
 
 
-def partial_kernel(per, x_ref, g_ref, w_ref, o_ref):
-    tokens, width = x_ref.shape
-    columns = w_ref.shape[2]
+def center_kernel(x_ref, g_ref, o_ref, s_ref):
+    width = x_ref.shape[1]
     values = x_ref[...].astype(jnp.float32)
     middle = rounded(jnp.sum(values, axis=1, keepdims=True) / width)
     centered = values - middle
     total = jnp.sum(centered, axis=1, keepdims=True)
     square = jnp.sum(centered * centered, axis=1, keepdims=True)
+    o_ref[...] = (centered * g_ref[...].reshape(1, width)).astype(jnp.bfloat16)
+    s_ref[...] = with_statistics(jnp.zeros(s_ref.shape, jnp.float32), (middle, total, square))
+
+
+def partial_kernel(per, x_ref, s_ref, g_ref, w_ref, o_ref):
+    tokens, width = x_ref.shape
+    columns = w_ref.shape[2]
     gain = g_ref[...].reshape(1, width)
-    scaled = (centered * gain).astype(jnp.bfloat16)
+    scaled = x_ref[...]
     high = rounded(gain)
     line = lax.broadcasted_iota(jnp.int32, (16, width), 0)
     gains = jnp.where(line == 0, high, jnp.where(line == 1, gain - high, 0.0)).astype(jnp.bfloat16)
@@ -71,7 +75,10 @@
             sums = jnp.where(row == chunks + chunk, pltpu.roll(piece, HALF, 1), sums)
             chunk += 1
     base = jnp.concatenate([sums] * (tokens // per), axis=0)
-    o_ref[:, 3 * columns :] = with_statistics(base, (middle, total, square))
+    upper = lax.broadcasted_iota(jnp.int32, base.shape, 1) >= HALF
+    o_ref[:, 3 * columns :] = jnp.where(upper, base, s_ref[...].astype(jnp.float32)).astype(
+        jnp.bfloat16
+    )
 
 
 def vector_sums(extras, chunks):
@@ -191,12 +198,21 @@
     size = count // CLASSES
     per = size // len(FAR[0])
     wide = 3 * columns + EXTRA
+    scaled, kept = pl.pallas_call(
+        center_kernel,
+        out_shape=[like((count, width)), like((count, EXTRA))],
+        name="center",
+        compiler_params=LIMIT,
+        cost_estimate=pl.CostEstimate(
+            flops=2 * 10**9, bytes_accessed=4 * count * width, transcendentals=0
+        ),
+    )(tokens, norm_gain)
     payload = pl.pallas_call(
         lambda *refs: partial_kernel(per, *refs),
         out_shape=like((count, wide)),
         name="partial",
-        compiler_params=FIRST,
-    )(tokens, norm_gain, jnp.transpose(qkv_weight, (1, 0, 2)))
+        compiler_params=LIMIT,
+    )(scaled, kept, norm_gain, jnp.transpose(qkv_weight, (1, 0, 2)))
     near = exchange(payload.reshape(CLASSES, size, wide), "row", NEAR)
     merged = pl.pallas_call(
         lambda *refs: merge_kernel(per, width, *refs),
@@ -215,8 +231,8 @@
     qkv = spread(block, "row", NEAR).reshape(count, 3 * columns)
     send = lax.ppermute(attend(True, qkv, out_weight), "col", CORES)
     pair = added(attend(False, qkv, out_weight), send)
-    four = added(pair, lax.ppermute(pair, "col", RIGHT))
-    half = added(four, lax.ppermute(four, "col", LEFT))
+    terms = spread(pair, "col", CHIPS)
+    half = jnp.sum(terms.astype(jnp.float32), axis=0).astype(jnp.bfloat16)
     rest = lax.ppermute(half, "col", CORES)
     core = lax.rem(lax.axis_index("col"), 2)
     return jnp.concatenate(

time: 93.2 us -> 90.6 us (0.972)
  blocking collectives: 56.2 us -> 69.7 us
  starting transfers between devices: 19.2 us -> 11.4 us
  waiting for transfers between devices: 8.38 us -> 0.98 us
  local copies, waits for them, and re-layouts: 2.9 us -> 1.87 us
    all_to_all x4 -> x5, blocking collectives: 56.2 us -> 69.7 us  [exchange(): return lax.all_to_all(a, axis, 0, 0, tiled=True, axis_index_groups=groups)]
    ppermute x2 -> x0, starting transfers between devices: 7.53 us -> none  [the longest x1 4.39 us: shards(): half = added(four, lax.ppermute(four, 'col', LEFT))]
    ppermute x2 -> x0, waiting for transfers between devices: 7.39 us -> none  [the longest x1 4.15 us: shards(): four = added(pair, lax.ppermute(pair, 'col', RIGHT))]
    unnamed x8, local copies, waits for them, and re-layouts: 2.82 us -> 1.73 us
  transfers between devices with their start and end apart: 4 -> 2, of which waited for: 3 -> 1; matrix products, arithmetic and copies ran while one was open for 0% -> 0% of each run, Pallas kernels for 2% -> 2%
where the time goes in v2:
time: 90.6 us; the launch traced here: 90.2 us
  blocking collectives  69.7 us (77%)
  starting transfers between devices  11.4 us (13%)
  Pallas kernels  5.26 us (6%)
  local copies, waits for them, and re-layouts  1.87 us (2%)
  waiting for transfers between devices  0.98 us (1%)
  other arithmetic  0.91 us (1%)
    all_to_all x5, blocking collectives, exchange(): return lax.all_to_all(a, axis, 0, 0, tiled=True, axis_index_groups=groups)  69.7 us
    ppermute x1, starting transfers between devices, shards(): send = lax.ppermute(attend(True, qkv, out_weight), 'col', CORES)  8.03 us
    ppermute x1, starting transfers between devices, shards(): rest = lax.ppermute(half, 'col', CORES)  3.35 us
    pallas_call x2, Pallas kernels, attend(): pl.pallas_call(lambda *refs: attend_kernel(other, *refs), out_shape=like(...  2.78 us
  transfers between devices with their start and end apart: 2, of which 1 were waited for; matrix products, arithmetic and copies ran while one was open for 0% of the time, Pallas kernels for 2%

profile of v2, /device:TPU:1, one launch (start us, length us, event | category | flops | bytes accessed | tf_op | source)
XLA Modules:
  0.0 90.2 jit_solution(10539896963532979896)
XLA Ops:
  0.0 0.0 copy-start
  0.0 0.0 copy-start.1
  0.0 0.8 copy-done.1
  0.8 0.0 copy-start.2
  0.8 1.0 %copy-done.2 = bf16[384,384]{1,0:T(8,128)(2,1)S(1)} copy-done((bf16[384,384]{1,0:T(8,128)(2,1)S(1)}, bf16[384,384]{1,0:T(8,128)(2,1)}, u32[]{:S(2)}) %copy-start.2) | copy-done | bytes 294936
  1.7 0.3 center.1
  2.0 0.0 copy-done
  2.1 1.0 %partial.1 = bf16[384,1280]{1,0:T(8,128)(2,1)S(1)} custom-call(bf16[384,384]{1,0:T(8,128)(2,1)S(1)} %get-tuple-element.7.refs_0_, bf16[384,128]{1,0:T(8,128)(2,1)S(1)} %get-tuple-element.8.refs_1_, f32[384]{0:T(512)S(1)} %copy-done.1, bf16[3,384,384]{2,1,0:T(8,128)(2,1)S(1)} %bitcast.7), custom_call_target="tpu_custom_call" | custom-call | tf_op jit(solution)/shard_map/partial/pallas_call | solution.py:210
  3.0 14.2 %all_to_all.25.refs_0_ = bf16[4,96,1280]{2,1,0:T(8,128)(2,1)S(1)} all-to-all(bf16[4,96,1280]{2,1,0:T(8,128)(2,1)S(1)} %bitcast.5), channel_id=1, replica_groups={{0,32,256,288},{64,96,320,352},{128,160,384,416},{192,224,448,480},{1,3..., dimensions={0} | all-to-all | bytes 1966080 | tf_op jit(solution)/shard_map/all_to_all | solution.py:184
  17.2 0.9 merge.1
  18.1 20.7 %all_to_all.26.refs_0_ = bf16[4,24,1280]{2,1,0:T(8,128)(2,1)S(1)} all-to-all(bf16[4,24,1280]{2,1,0:T(8,128)(2,1)S(1)} %bitcast.6), channel_id=1, replica_groups={{0,64,128,192},{32,96,160,224},{256,320,384,448},{288,352,416,480},{1,6..., dimensions={0} | all-to-all | bytes 491520 | tf_op jit(solution)/shard_map/all_to_all | solution.py:184
  38.8 0.3 norm.1
  39.2 10.5 %all_to_all.27 = bf16[4,24,1152]{2,1,0:T(8,128)(2,1)S(1)} all-to-all(bf16[4,24,1152]{2,1,0:T(8,128)(2,1)S(1)} %broadcast_in_dim.8), channel_id=1, replica_groups={{0,64,128,192},{32,96,160,224},{256,320,384,448},{288,352,416,480},{1,6..., dimensions={0} | all-to-all | bytes 442368 | tf_op jit(solution)/shard_map/all_to_all | solution.py:184
  49.7 0.1 broadcast_in_dim.10
  49.8 0.0 copy-start.3
  49.8 10.8 %all_to_all.28 = bf16[4,96,1152]{2,1,0:T(8,128)(2,1)S(1)} all-to-all(bf16[4,96,1152]{2,1,0:T(8,128)(2,1)S(1)} %broadcast_in_dim.10), channel_id=1, replica_groups={{0,32,256,288},{64,96,320,352},{128,160,384,416},{192,224,448,480},{1,3..., dimensions={0} | all-to-all | bytes 1769472 | tf_op jit(solution)/shard_map/all_to_all | solution.py:184
  60.6 0.0 copy-done.3
  60.6 1.4 %attend.3 = bf16[192,384]{1,0:T(8,128)(2,1)S(1)} custom-call(bf16[384,1152]{1,0:T(8,128)(2,1)S(1)} %bitcast.8, bf16[384,384]{1,0:T(8,128)(2,1)S(1)} %copy-done.3), custom_call_target="tpu_custom_call" | custom-call | flops 679477248 | bytes 884736 | tf_op jit(solution)/shard_map/attend/pallas_call | solution.py:168
  62.0 8.0 %collective-permute-start = (bf16[192,384]{1,0:T(8,128)(2,1)S(1)}, bf16[192,384]{1,0:T(8,128)(2,1)S(1)}, u32[]{:S(2)}, u32[]{:S(2)}) collective-permute-start(bf16[192,384]{1,0:T(8,128)(2,1)S(1)} %attend.3), channel_id=1, source_target_pairs={{0,4},{4,0},{8,12},{12,8},{16,20},{20,16},{24,28},{28,24},{1,5},{5... | collective-permute-start | bytes 442376 | tf_op jit(solution)/shard_map/ppermute | solution.py:232
  70.0 1.4 %attend.2 = bf16[192,384]{1,0:T(8,128)(2,1)S(1)} custom-call(bf16[384,1152]{1,0:T(8,128)(2,1)S(1)} %bitcast.9, bf16[384,384]{1,0:T(8,128)(2,1)S(1)} %copy-done.3), custom_call_target="tpu_custom_call" | custom-call | flops 679477248 | bytes 884736 | tf_op jit(solution)/shard_map/attend/pallas_call | solution.py:168
  71.4 0.0 collective-permute-done
  71.4 0.1 broadcast_in_dim.22
  71.5 13.5 %all_to_all.29 = bf16[4,192,384]{2,1,0:T(8,128)(2,1)S(1)} all-to-all(bf16[4,192,384]{2,1,0:T(8,128)(2,1)S(1)} %broadcast_in_dim.22), channel_id=1, replica_groups={{0,8,16,24},{4,12,20,28},{1,9,17,25},{5,13,21,29},{2,10,18,26},{6,14,22..., dimensions={0} | all-to-all | bytes 1179648 | tf_op jit(solution)/shard_map/all_to_all | solution.py:184
  85.0 0.1 reduce_sum.12
  85.1 3.4 %collective-permute-start.1 = (bf16[192,384]{1,0:T(8,128)(2,1)S(1)}, bf16[192,384]{1,0:T(8,128)(2,1)S(1)}, u32[]{:S(2)}, u32[]{:S(2)}) collective-permute-start(bf16[192,384]{1,0:T(8,128)(2,1)S(1)} %reduce_sum.12), channel_id=1, source_target_pairs={{0,4},{4,0},{8,12},{12,8},{16,20},{20,16},{24,28},{28,24},{1,5},{5... | collective-permute-start | bytes 442376 | tf_op jit(solution)/shard_map/ppermute | solution.py:236
  88.5 1.0 %collective-permute-done.1 = bf16[192,384]{1,0:T(8,128)(2,1)S(1)} collective-permute-done((bf16[192,384]{1,0:T(8,128)(2,1)S(1)}, bf16[192,384]{1,0:T(8,128)(2,1)S(1)}, u32[]{:S(2)}, u32[]{:S(2)}) %collective-permute-start.1) | collective-permute-done | bytes 147488 | tf_op jit(solution)/shard_map/ppermute | solution.py:236
  89.5 0.7 pad_maximum_fusion
  (3 shorter events, 0.1 us)
Async XLA Ops:
  0.0 2.0 %copy-start = (bf16[384,3,384]{2,0,1:T(8,128)(2,1)S(1)}, bf16[384,3,384]{2,0,1:T(8,128)(2,1)}, u32[]{:S(2)}) copy-start(bf16[384,3,384]{2,0,1:T(8,128)(2,1)} %param.6) | copy-start | bytes 2654212
  0.0 0.8 copy-start.1
  0.8 1.0 %copy-start.2 = (bf16[384,384]{1,0:T(8,128)(2,1)S(1)}, bf16[384,384]{1,0:T(8,128)(2,1)}, u32[]{:S(2)}) copy-start(bf16[384,384]{1,0:T(8,128)(2,1)} %x_ref.1) | copy-start | bytes 884740
  49.8 10.8 %copy-start.3 = (bf16[384,384]{1,0:T(8,128)(2,1)S(1)}, bf16[384,384]{1,0:T(8,128)(2,1)}, u32[]{:S(2)}) copy-start(bf16[384,384]{1,0:T(8,128)(2,1)} %refs_1_.3) | copy-start | bytes 884740
  62.0 9.4 %collective-permute-start = (bf16[192,384]{1,0:T(8,128)(2,1)S(1)}, bf16[192,384]{1,0:T(8,128)(2,1)S(1)}, u32[]{:S(2)}, u32[]{:S(2)}) collective-permute-start(bf16[192,384]{1,0:T(8,128)(2,1)S(1)} %attend.3), channel_id=1, source_target_pairs={{0,4},{4,0},{8,12},{12,8},{16,20},{20,16},{24,28},{28,24},{1,5},{5... | collective-permute-start | bytes 442376 | tf_op jit(solution)/shard_map/ppermute | solution.py:232
  85.1 4.3 %collective-permute-start.1 = (bf16[192,384]{1,0:T(8,128)(2,1)S(1)}, bf16[192,384]{1,0:T(8,128)(2,1)S(1)}, u32[]{:S(2)}, u32[]{:S(2)}) collective-permute-start(bf16[192,384]{1,0:T(8,128)(2,1)S(1)} %reduce_sum.12), channel_id=1, source_target_pairs={{0,4},{4,0},{8,12},{12,8},{16,20},{20,16},{24,28},{28,24},{1,5},{5... | collective-permute-start | bytes 442376 | tf_op jit(solution)/shard_map/ppermute | solution.py:236

commit v3 on v2

v3 whole, which is shorter than its diff:
```python
import math

import jax
import jax.numpy as jnp
from jax import lax
from jax.experimental import pallas as pl
from jax.experimental.pallas import tpu as pltpu
from jax.sharding import PartitionSpec as P

K = 128
EPSILON = 1e-05
LANES = 128
HALF = 64
GROUP = 8
FIELDS = 5
TAIL = 16
LIMIT = pltpu.CompilerParams(vmem_limit_bytes=20 * 2**20)

CLASSES = 4
NEAR = [[8 * y + 2 * i + b for y in range(2) for b in range(2)] for i in range(4)]
FAR = [[8 * y + 2 * i + b for i in range(4)] for y in range(2) for b in range(2)]
CORES = [(c, c ^ 1) for c in range(8)]
CHIPS = [[0, 2, 4, 6], [1, 3, 5, 7]]


def rounded(a):
    return a.astype(jnp.bfloat16).astype(jnp.float32)


def dot32(a, b):
    return jnp.dot(a, b, preferred_element_type=jnp.float32)


def packed(columns):
    middle, total, square = columns
    tokens = middle.shape[0]
    fields = (
        middle, rounded(total), total - rounded(total), rounded(square), square - rounded(square)
    )
    lane = lax.broadcasted_iota(jnp.int32, (GROUP, LANES), 1)
    tile = jnp.zeros((GROUP, LANES), jnp.float32)
    for group in range(tokens // GROUP):
        for at, field in enumerate(fields):
            tile = jnp.where(
                lane == group * FIELDS + at, field[group * GROUP : (group + 1) * GROUP], tile
            )
    return tile


def unpacked(tile, tokens):
    groups = [
        tile if group == 0 else pltpu.roll(tile, LANES - group * FIELDS, 1)
        for group in range(tokens // GROUP)
    ]
    lines = jnp.concatenate(groups, axis=0)
    return lines[:, 0:1], lines[:, 1:2] + lines[:, 2:3], lines[:, 3:4] + lines[:, 4:5]


def tail_of(tile, sums):
    row = lax.broadcasted_iota(jnp.int32, (GROUP, LANES), 0)
    lane = lax.broadcasted_iota(jnp.int32, (GROUP, LANES), 1)
    first = jnp.zeros((GROUP, LANES), jnp.float32)
    for at in range(GROUP):
        first = jnp.where(row == at, sums[at], first)
    last = sums[GROUP]
    turned = pltpu.roll(last, HALF, 1)
    second = jnp.where(lane < HALF, tile, jnp.where(row == 0, last, turned))
    return jnp.concatenate([first, second], axis=0)


def sums_of(tail):
    upper = lax.broadcasted_iota(jnp.int32, (1, LANES), 1) >= HALF
    second = tail[GROUP:]
    turned = pltpu.roll(second, HALF, 1)
    return [tail[at : at + 1] for at in range(GROUP)] + [
        jnp.where(upper, second[0:1], turned[1:2])
    ]


def center_kernel(x_ref, o_ref, s_ref):
    count, width = x_ref.shape
    values = x_ref[...].astype(jnp.float32)
    middle = rounded(jnp.sum(values, axis=1, keepdims=True) / width)
    centered = values - middle
    total = jnp.sum(centered, axis=1, keepdims=True)
    square = jnp.sum(centered * centered, axis=1, keepdims=True)
    o_ref[...] = centered
    size = count // CLASSES
    for block in range(CLASSES):
        lines = slice(block * size, (block + 1) * size)
        s_ref[block] = packed((middle[lines], total[lines], square[lines]))


def partial_kernel(x_ref, s_ref, g_ref, w_ref, o_ref):
    tokens, width = x_ref.shape
    size = tokens // CLASSES
    columns = w_ref.shape[2]
    gain = g_ref[...].reshape(1, width)
    scaled = (x_ref[...] * gain).astype(jnp.bfloat16)
    high = rounded(gain)
    line = lax.broadcasted_iota(jnp.int32, (16, width), 0)
    gains = jnp.where(line == 0, high, jnp.where(line == 1, gain - high, 0.0)).astype(jnp.bfloat16)
    sums = []
    for part in range(3):
        weight = w_ref[part]
        product = dot32(scaled, weight).astype(jnp.bfloat16)
        c = jnp.sum(dot32(gains, weight), axis=0, keepdims=True)
        for at in range(0, columns, LANES):
            to = len(sums) * size
            for block in range(CLASSES):
                o_ref[block, to : to + size, :] = product[
                    block * size : (block + 1) * size, at : at + LANES
                ]
            sums.append(c[:, at : at + LANES])
    for block in range(CLASSES):
        o_ref[block, len(sums) * size :, :] = tail_of(s_ref[block], sums).astype(jnp.bfloat16)


def merge_kernel(width, r_ref, o_ref):
    blocks = r_ref.shape[0]
    members, rows, _ = o_ref.shape
    chunks = GROUP + 1
    per = (rows - TAIL) // chunks
    size = per * members
    tails = [r_ref[d, chunks * size :, :].astype(jnp.float32) for d in range(blocks)]
    held = [unpacked(t[GROUP:], size) for t in tails]
    middle = rounded(sum(m + t / width for m, t, _ in held) / blocks)
    shifts = [m - middle for m, _, _ in held]
    total = sum(t + width * s for s, (_, t, _) in zip(shifts, held))
    square = sum(q + 2.0 * s * t + width * (s * s) for s, (_, t, q) in zip(shifts, held))
    sums = [sums_of(t) for t in tails]
    wide = [jnp.broadcast_to(s, (size, LANES)) for s in shifts]
    for at in range(chunks):
        running = jnp.zeros((size, LANES), jnp.float32)
        for d in range(blocks):
            term = r_ref[d, at * size : (at + 1) * size, :].astype(jnp.float32)
            running = running + term + wide[d] * sums[d][at]
        result = running.astype(jnp.bfloat16)
        for member in range(members):
            o_ref[member, at * per : (at + 1) * per, :] = result[member * per : (member + 1) * per]
    merged = [sum(s[at] for s in sums) for at in range(chunks)]
    for member in range(members):
        lines = slice(member * per, (member + 1) * per)
        tile = packed((middle[lines], total[lines], square[lines]))
        o_ref[member, chunks * per :, :] = tail_of(tile, merged).astype(jnp.bfloat16)


def norm_kernel(width, r_ref, o_ref):
    blocks = r_ref.shape[0]
    per, columns = o_ref.shape
    chunks = columns // LANES
    tails = [r_ref[d, chunks * per :, :].astype(jnp.float32) for d in range(blocks)]
    held = [unpacked(t[GROUP:], per) for t in tails]
    average = sum(m + t / width for m, t, _ in held) / blocks
    shifts = [m - average for m, _, _ in held]
    variance = sum(
        q + 2.0 * s * t + width * (s * s) for s, (_, t, q) in zip(shifts, held)
    ) / (width * blocks)
    scale = lax.rsqrt(variance + EPSILON)
    wide = [jnp.broadcast_to(s, (per, LANES)) for s in shifts]
    sums = [sums_of(t) for t in tails]
    for at in range(chunks):
        running = jnp.zeros((per, LANES), jnp.float32)
        for d in range(blocks):
            term = r_ref[d, at * per : (at + 1) * per, :].astype(jnp.float32)
            running = running + term + wide[d] * sums[d][at]
        o_ref[:, at * LANES : (at + 1) * LANES] = (running * scale).astype(jnp.bfloat16)


def attend_kernel(other, x_ref, w_ref, o_ref):
    columns = w_ref.shape[0]
    half = o_ref.shape[0]
    core = lax.rem(lax.axis_index("col"), 2)
    which = 1 - core if other else core
    lines = pl.ds(pl.multiple_of(which * half, half), half)
    scaling = 1.0 / math.sqrt(K)
    outs = []
    for at in range(0, columns, K):
        q = x_ref[lines, at : at + K]
        k = x_ref[:, columns + at : columns + at + K]
        v = x_ref[:, 2 * columns + at : 2 * columns + at + K]
        scores = (
            lax.dot_general(q, k, (((1,), (1,)), ((), ())), preferred_element_type=jnp.float32)
            * scaling
        )
        largest = jnp.max(scores, axis=1, keepdims=True)
        exponent = jnp.exp(scores - largest)
        inverse = 1.0 / jnp.sum(exponent, axis=1, keepdims=True)
        outs.append(dot32((exponent * inverse).astype(jnp.bfloat16), v).astype(jnp.bfloat16))
    o_ref[...] = dot32(jnp.concatenate(outs, axis=1), w_ref[...]).astype(jnp.bfloat16)


def attend(other, qkv, weight):
    count, wide = qkv.shape
    width = weight.shape[1]
    flops = 2 * (count // 2) * (2 * count * weight.shape[0] + weight.shape[0] * width)
    return pl.pallas_call(
        lambda *refs: attend_kernel(other, *refs),
        out_shape=like((count // 2, width)),
        name="attend",
        compiler_params=LIMIT,
        cost_estimate=pl.CostEstimate(
            flops=4 * flops, bytes_accessed=2 * count * wide, transcendentals=0
        ),
    )(qkv, weight)


def added(a, b):
    return (a.astype(jnp.float32) + b.astype(jnp.float32)).astype(jnp.bfloat16)


def exchange(a, axis, groups):
    return lax.all_to_all(a, axis, 0, 0, tiled=True, axis_index_groups=groups)


def spread(a, axis, groups):
    return exchange(jnp.broadcast_to(a[None], (len(groups[0]), *a.shape)), axis, groups)


def like(shape):
    return jax.ShapeDtypeStruct(shape, jnp.bfloat16)


def shards(tokens, norm_gain, qkv_weight, out_weight):
    count, width = tokens.shape
    columns = qkv_weight.shape[2]
    size = count // CLASSES
    per = size // len(FAR[0])
    chunks = GROUP + 1
    centered, kept = pl.pallas_call(
        center_kernel,
        out_shape=[
            jax.ShapeDtypeStruct((count, width), jnp.float32),
            jax.ShapeDtypeStruct((CLASSES, GROUP, LANES), jnp.float32),
        ],
        name="center",
        compiler_params=LIMIT,
        cost_estimate=pl.CostEstimate(
            flops=2 * 10**9, bytes_accessed=4 * count * width, transcendentals=0
        ),
    )(tokens)
    payload = pl.pallas_call(
        partial_kernel,
        out_shape=like((CLASSES, chunks * size + TAIL, LANES)),
        name="partial",
        compiler_params=LIMIT,
    )(centered, kept, norm_gain, jnp.transpose(qkv_weight, (1, 0, 2)))
    near = exchange(payload, "row", NEAR)
    merged = pl.pallas_call(
        lambda *refs: merge_kernel(width, *refs),
        out_shape=like((len(FAR[0]), chunks * per + TAIL, LANES)),
        name="merge",
        compiler_params=LIMIT,
    )(near)
    far = exchange(merged, "row", FAR)
    mine = pl.pallas_call(
        lambda *refs: norm_kernel(width * CLASSES, *refs),
        out_shape=like((per, 3 * columns)),
        name="norm",
        compiler_params=LIMIT,
    )(far)
    block = spread(mine, "row", FAR).reshape(size, 3 * columns)
    qkv = spread(block, "row", NEAR).reshape(count, 3 * columns)
    send = lax.ppermute(attend(True, qkv, out_weight), "col", CORES)
    pair = added(attend(False, qkv, out_weight), send)
    terms = spread(pair, "col", CHIPS)
    half = jnp.sum(terms.astype(jnp.float32), axis=0).astype(jnp.bfloat16)
    rest = lax.ppermute(half, "col", CORES)
    core = lax.rem(lax.axis_index("col"), 2)
    return jnp.concatenate(
        [jnp.where(core == 0, half, rest), jnp.where(core == 0, rest, half)], axis=0
    )


def solution(mesh):
    in_specs = (P("dp", "row"), P("row"), P("row", None, "col"), P("col", "row"))
    out_specs = P("dp", "row")
    return jax.shard_map(shards, mesh=mesh, in_specs=in_specs, out_specs=out_specs, check_vma=False)
```

time: 90.6 us -> 89.7 us (0.990)
  blocking collectives: 69.7 us -> 68.5 us
    all_to_all x5, blocking collectives: 69.7 us -> 68.5 us  [exchange(): return lax.all_to_all(a, axis, 0, 0, tiled=True, axis_index_groups=groups)]
where the time goes in v3:
time: 89.7 us; the launch traced here: 89.3 us
  blocking collectives  68.5 us (76%)
  starting transfers between devices  11.6 us (13%)
  Pallas kernels  5.33 us (6%)
  local copies, waits for them, and re-layouts  1.85 us (2%)
  waiting for transfers between devices  0.98 us (1%)
  other arithmetic  0.91 us (1%)
    all_to_all x5, blocking collectives, exchange(): return lax.all_to_all(a, axis, 0, 0, tiled=True, axis_index_groups=groups)  68.5 us
    ppermute x1, starting transfers between devices, shards(): send = lax.ppermute(attend(True, qkv, out_weight), 'col', CORES)  8.27 us
    ppermute x1, starting transfers between devices, shards(): rest = lax.ppermute(half, 'col', CORES)  3.35 us
    pallas_call x2, Pallas kernels, attend(): pl.pallas_call(lambda *refs: attend_kernel(other, *refs), out_shape=like(...  2.78 us
  transfers between devices with their start and end apart: 2, of which 1 were waited for; matrix products, arithmetic and copies ran while one was open for 0% of the time, Pallas kernels for 2%

profile of v3, /device:TPU:1, one launch (start us, length us, event | category | flops | bytes accessed | tf_op | source)
XLA Modules:
  0.0 89.3 jit_solution(14436038130627541875)
XLA Ops:
  0.0 0.0 copy-start
  0.0 0.0 copy-start.2
  0.0 1.0 %copy-done.2 = bf16[384,384]{1,0:T(8,128)(2,1)S(1)} copy-done((bf16[384,384]{1,0:T(8,128)(2,1)S(1)}, bf16[384,384]{1,0:T(8,128)(2,1)}, u32[]{:S(2)}) %copy-start.2) | copy-done | bytes 294936
  1.0 0.3 center.1
  1.3 0.0 copy-start.1
  1.3 0.0 copy-done
  1.4 0.7 copy-done.1
  2.0 0.9 %partial.1 = bf16[4,880,128]{2,1,0:T(8,128)(2,1)S(1)} custom-call(f32[384,384]{1,0:T(8,128)S(1)} %get-tuple-element.7.x_ref, f32[4,8,128]{2,1,0:T(8,128)S(1)} %get-tuple-element.8.s_ref, f32[384]{0:T(512)S(1)} %copy-done.1, bf16[3,384,384]{2,1,0:T(8,128)(2,1)S(1)} %bitcast.5), custom_call_target="tpu_custom_call" | custom-call | tf_op jit(solution)/shard_map/partial/pallas_call | solution.py:242
  3.0 13.0 %all_to_all.25.refs_0_ = bf16[4,880,128]{2,1,0:T(8,128)(2,1)S(1)} all-to-all(bf16[4,880,128]{2,1,0:T(8,128)(2,1)S(1)} %partial.1), channel_id=1, replica_groups={{0,32,256,288},{64,96,320,352},{128,160,384,416},{192,224,448,480},{1,3..., dimensions={0} | all-to-all | bytes 1802240 | tf_op jit(solution)/shard_map/all_to_all | solution.py:213
  16.0 0.9 %merge.1 = bf16[4,232,128]{2,1,0:T(8,128)(2,1)S(1)} custom-call(bf16[4,880,128]{2,1,0:T(8,128)(2,1)S(1)} %all_to_all.25.refs_0_), custom_call_target="tpu_custom_call" | custom-call | tf_op jit(solution)/shard_map/merge/pallas_call | solution.py:249
  16.9 20.8 %all_to_all.26.refs_0_ = bf16[4,232,128]{2,1,0:T(8,128)(2,1)S(1)} all-to-all(bf16[4,232,128]{2,1,0:T(8,128)(2,1)S(1)} %merge.1), channel_id=1, replica_groups={{0,64,128,192},{32,96,160,224},{256,320,384,448},{288,352,416,480},{1,6..., dimensions={0} | all-to-all | bytes 475136 | tf_op jit(solution)/shard_map/all_to_all | solution.py:213
  37.8 0.4 norm.1
  38.2 10.6 %all_to_all.27 = bf16[4,24,1152]{2,1,0:T(8,128)(2,1)S(1)} all-to-all(bf16[4,24,1152]{2,1,0:T(8,128)(2,1)S(1)} %broadcast_in_dim.8), channel_id=1, replica_groups={{0,64,128,192},{32,96,160,224},{256,320,384,448},{288,352,416,480},{1,6..., dimensions={0} | all-to-all | bytes 442368 | tf_op jit(solution)/shard_map/all_to_all | solution.py:213
  48.8 0.1 broadcast_in_dim.10
  48.9 0.0 copy-start.3
  48.9 10.5 %all_to_all.28 = bf16[4,96,1152]{2,1,0:T(8,128)(2,1)S(1)} all-to-all(bf16[4,96,1152]{2,1,0:T(8,128)(2,1)S(1)} %broadcast_in_dim.10), channel_id=1, replica_groups={{0,32,256,288},{64,96,320,352},{128,160,384,416},{192,224,448,480},{1,3..., dimensions={0} | all-to-all | bytes 1769472 | tf_op jit(solution)/shard_map/all_to_all | solution.py:213
  59.4 0.0 copy-done.3
  59.4 1.4 %attend.3 = bf16[192,384]{1,0:T(8,128)(2,1)S(1)} custom-call(bf16[384,1152]{1,0:T(8,128)(2,1)S(1)} %bitcast.3, bf16[384,384]{1,0:T(8,128)(2,1)S(1)} %copy-done.3), custom_call_target="tpu_custom_call" | custom-call | flops 679477248 | bytes 884736 | tf_op jit(solution)/shard_map/attend/pallas_call | solution.py:197
  60.8 8.3 %collective-permute-start = (bf16[192,384]{1,0:T(8,128)(2,1)S(1)}, bf16[192,384]{1,0:T(8,128)(2,1)S(1)}, u32[]{:S(2)}, u32[]{:S(2)}) collective-permute-start(bf16[192,384]{1,0:T(8,128)(2,1)S(1)} %attend.3), channel_id=1, source_target_pairs={{0,4},{4,0},{8,12},{12,8},{16,20},{20,16},{24,28},{28,24},{1,5},{5... | collective-permute-start | bytes 442376 | tf_op jit(solution)/shard_map/ppermute | solution.py:264
  69.1 1.4 %attend.2 = bf16[192,384]{1,0:T(8,128)(2,1)S(1)} custom-call(bf16[384,1152]{1,0:T(8,128)(2,1)S(1)} %bitcast.4, bf16[384,384]{1,0:T(8,128)(2,1)S(1)} %copy-done.3), custom_call_target="tpu_custom_call" | custom-call | flops 679477248 | bytes 884736 | tf_op jit(solution)/shard_map/attend/pallas_call | solution.py:197
  70.5 0.0 collective-permute-done
  70.6 0.1 broadcast_in_dim.22
  70.6 13.5 %all_to_all.29 = bf16[4,192,384]{2,1,0:T(8,128)(2,1)S(1)} all-to-all(bf16[4,192,384]{2,1,0:T(8,128)(2,1)S(1)} %broadcast_in_dim.22), channel_id=1, replica_groups={{0,8,16,24},{4,12,20,28},{1,9,17,25},{5,13,21,29},{2,10,18,26},{6,14,22..., dimensions={0} | all-to-all | bytes 1179648 | tf_op jit(solution)/shard_map/all_to_all | solution.py:213
  84.1 0.1 reduce_sum.12
  84.2 3.4 %collective-permute-start.1 = (bf16[192,384]{1,0:T(8,128)(2,1)S(1)}, bf16[192,384]{1,0:T(8,128)(2,1)S(1)}, u32[]{:S(2)}, u32[]{:S(2)}) collective-permute-start(bf16[192,384]{1,0:T(8,128)(2,1)S(1)} %reduce_sum.12), channel_id=1, source_target_pairs={{0,4},{4,0},{8,12},{12,8},{16,20},{20,16},{24,28},{28,24},{1,5},{5... | collective-permute-start | bytes 442376 | tf_op jit(solution)/shard_map/ppermute | solution.py:268
  87.6 1.0 %collective-permute-done.1 = bf16[192,384]{1,0:T(8,128)(2,1)S(1)} collective-permute-done((bf16[192,384]{1,0:T(8,128)(2,1)S(1)}, bf16[192,384]{1,0:T(8,128)(2,1)S(1)}, u32[]{:S(2)}, u32[]{:S(2)}) %collective-permute-start.1) | collective-permute-done | bytes 147488 | tf_op jit(solution)/shard_map/ppermute | solution.py:268
  88.6 0.7 pad_maximum_fusion
  (3 shorter events, 0.1 us)
Async XLA Ops:
  0.0 1.3 %copy-start = (bf16[384,3,384]{2,0,1:T(8,128)(2,1)S(1)}, bf16[384,3,384]{2,0,1:T(8,128)(2,1)}, u32[]{:S(2)}) copy-start(bf16[384,3,384]{2,0,1:T(8,128)(2,1)} %param.6) | copy-start | bytes 2654212
  0.0 1.0 %copy-start.2 = (bf16[384,384]{1,0:T(8,128)(2,1)S(1)}, bf16[384,384]{1,0:T(8,128)(2,1)}, u32[]{:S(2)}) copy-start(bf16[384,384]{1,0:T(8,128)(2,1)} %x_ref.1) | copy-start | bytes 884740
  1.3 0.7 copy-start.1
  48.9 10.6 %copy-start.3 = (bf16[384,384]{1,0:T(8,128)(2,1)S(1)}, bf16[384,384]{1,0:T(8,128)(2,1)}, u32[]{:S(2)}) copy-start(bf16[384,384]{1,0:T(8,128)(2,1)} %refs_1_.3) | copy-start | bytes 884740
  60.8 9.7 %collective-permute-start = (bf16[192,384]{1,0:T(8,128)(2,1)S(1)}, bf16[192,384]{1,0:T(8,128)(2,1)S(1)}, u32[]{:S(2)}, u32[]{:S(2)}) collective-permute-start(bf16[192,384]{1,0:T(8,128)(2,1)S(1)} %attend.3), channel_id=1, source_target_pairs={{0,4},{4,0},{8,12},{12,8},{16,20},{20,16},{24,28},{28,24},{1,5},{5... | collective-permute-start | bytes 442376 | tf_op jit(solution)/shard_map/ppermute | solution.py:264
  84.2 4.3 %collective-permute-start.1 = (bf16[192,384]{1,0:T(8,128)(2,1)S(1)}, bf16[192,384]{1,0:T(8,128)(2,1)S(1)}, u32[]{:S(2)}, u32[]{:S(2)}) collective-permute-start(bf16[192,384]{1,0:T(8,128)(2,1)S(1)} %reduce_sum.12), channel_id=1, source_target_pairs={{0,4},{4,0},{8,12},{12,8},{16,20},{20,16},{24,28},{28,24},{1,5},{5... | collective-permute-start | bytes 442376 | tf_op jit(solution)/shard_map/ppermute | solution.py:268

commit v4 on v3

--- a/solution.py
+++ b/solution.py
@@ -47,13 +47,33 @@
     return tile
 
 
-def unpacked(tile, tokens):
-    groups = [
-        tile if group == 0 else pltpu.roll(tile, LANES - group * FIELDS, 1)
-        for group in range(tokens // GROUP)
-    ]
-    lines = jnp.concatenate(groups, axis=0)
-    return lines[:, 0:1], lines[:, 1:2] + lines[:, 2:3], lines[:, 3:4] + lines[:, 4:5]
+def moved(tile, lanes):
+    return tile if lanes % LANES == 0 else pltpu.roll(tile, -lanes % LANES, 1)
+
+
+def held_in(tile):
+    return tile, moved(tile, 1) + moved(tile, 2), moved(tile, 3) + moved(tile, 4)
+
+
+def fields_of(middle, total, square):
+    lane = lax.broadcasted_iota(jnp.int32, (GROUP, LANES), 1)
+    field = lax.rem(lane, FIELDS)
+    tile = middle
+    for at, number in enumerate(
+        (rounded(total), total - rounded(total), rounded(square), square - rounded(square))
+    ):
+        tile = jnp.where(field == at + 1, moved(number, -1 - at), tile)
+    return jnp.where(lane < HALF, tile, 0.0)
+
+
+def lines_of(tile, tokens):
+    return jnp.concatenate(
+        [
+            jnp.broadcast_to(tile[:, group * FIELDS : group * FIELDS + 1], (GROUP, LANES))
+            for group in range(tokens // GROUP)
+        ],
+        axis=0,
+    )
 
 
 def tail_of(tile, sums):
@@ -123,13 +143,13 @@
     per = (rows - TAIL) // chunks
     size = per * members
     tails = [r_ref[d, chunks * size :, :].astype(jnp.float32) for d in range(blocks)]
-    held = [unpacked(t[GROUP:], size) for t in tails]
+    held = [held_in(t[GROUP:]) for t in tails]
     middle = rounded(sum(m + t / width for m, t, _ in held) / blocks)
     shifts = [m - middle for m, _, _ in held]
     total = sum(t + width * s for s, (_, t, _) in zip(shifts, held))
     square = sum(q + 2.0 * s * t + width * (s * s) for s, (_, t, q) in zip(shifts, held))
     sums = [sums_of(t) for t in tails]
-    wide = [jnp.broadcast_to(s, (size, LANES)) for s in shifts]
+    wide = [lines_of(s, size) for s in shifts]
     for at in range(chunks):
         running = jnp.zeros((size, LANES), jnp.float32)
         for d in range(blocks):
@@ -139,10 +159,10 @@
         for member in range(members):
             o_ref[member, at * per : (at + 1) * per, :] = result[member * per : (member + 1) * per]
     merged = [sum(s[at] for s in sums) for at in range(chunks)]
+    tile = fields_of(middle, total, square)
     for member in range(members):
-        lines = slice(member * per, (member + 1) * per)
-        tile = packed((middle[lines], total[lines], square[lines]))
-        o_ref[member, chunks * per :, :] = tail_of(tile, merged).astype(jnp.bfloat16)
+        part = moved(tile, member * (per // GROUP) * FIELDS)
+        o_ref[member, chunks * per :, :] = tail_of(part, merged).astype(jnp.bfloat16)
 
 
 def norm_kernel(width, r_ref, o_ref):
@@ -150,14 +170,14 @@
     per, columns = o_ref.shape
     chunks = columns // LANES
     tails = [r_ref[d, chunks * per :, :].astype(jnp.float32) for d in range(blocks)]
-    held = [unpacked(t[GROUP:], per) for t in tails]
+    held = [held_in(t[GROUP:]) for t in tails]
     average = sum(m + t / width for m, t, _ in held) / blocks
     shifts = [m - average for m, _, _ in held]
     variance = sum(
         q + 2.0 * s * t + width * (s * s) for s, (_, t, q) in zip(shifts, held)
     ) / (width * blocks)
-    scale = lax.rsqrt(variance + EPSILON)
-    wide = [jnp.broadcast_to(s, (per, LANES)) for s in shifts]
+    scale = lines_of(lax.rsqrt(variance + EPSILON), per)
+    wide = [lines_of(s, per) for s in shifts]
     sums = [sums_of(t) for t in tails]
     for at in range(chunks):
         running = jnp.zeros((per, LANES), jnp.float32)
@@ -174,19 +194,30 @@
     which = 1 - core if other else core
     lines = pl.ds(pl.multiple_of(which * half, half), half)
     scaling = 1.0 / math.sqrt(K)
-    outs = []
-    for at in range(0, columns, K):
-        q = x_ref[lines, at : at + K]
-        k = x_ref[:, columns + at : columns + at + K]
-        v = x_ref[:, 2 * columns + at : 2 * columns + at + K]
-        scores = (
-            lax.dot_general(q, k, (((1,), (1,)), ((), ())), preferred_element_type=jnp.float32)
-            * scaling
-        )
-        largest = jnp.max(scores, axis=1, keepdims=True)
-        exponent = jnp.exp(scores - largest)
-        inverse = 1.0 / jnp.sum(exponent, axis=1, keepdims=True)
-        outs.append(dot32((exponent * inverse).astype(jnp.bfloat16), v).astype(jnp.bfloat16))
+    starts = range(0, columns, K)
+    scores = jnp.concatenate(
+        [
+            lax.dot_general(
+                x_ref[lines, at : at + K],
+                x_ref[:, columns + at : columns + at + K],
+                (((1,), (1,)), ((), ())),
+                preferred_element_type=jnp.float32,
+            )
+            for at in starts
+        ],
+        axis=0,
+    )
+    largest = jnp.max(scores, axis=1, keepdims=True)
+    exponent = jnp.exp((scores - largest) * scaling)
+    inverse = 1.0 / jnp.sum(exponent, axis=1, keepdims=True)
+    shares = (exponent * inverse).astype(jnp.bfloat16)
+    outs = [
+        dot32(
+            shares[head * half : (head + 1) * half],
+            x_ref[:, 2 * columns + at : 2 * columns + at + K],
+        ).astype(jnp.bfloat16)
+        for head, at in enumerate(starts)
+    ]
     o_ref[...] = dot32(jnp.concatenate(outs, axis=1), w_ref[...]).astype(jnp.bfloat16)
 
 

time: 89.7 us -> 88 us (0.981)
  Pallas kernels: 5.33 us -> 3.48 us
    pallas_call x2, Pallas kernels: 2.78 us -> 1.66 us  [attend(): pl.pallas_call(lambda *refs: attend_kernel(other, *refs), out_shape=like(...]
  transfers between devices with their start and end apart: 2 -> 2, of which waited for: 1 -> 2; matrix products, arithmetic and copies ran while one was open for 0% -> 0% of each run, Pallas kernels for 2% -> 1%
where the time goes in v4:
time: 88 us; the launch traced here: 87.6 us
  blocking collectives  68.5 us (78%)
  starting transfers between devices  11.7 us (13%)
  Pallas kernels  3.48 us (4%)
  local copies, waits for them, and re-layouts  1.85 us (2%)
  waiting for transfers between devices  1.13 us (1%)
  other arithmetic  0.91 us (1%)
    all_to_all x5, blocking collectives, exchange(): return lax.all_to_all(a, axis, 0, 0, tiled=True, axis_index_groups=groups)  68.5 us
    ppermute x1, starting transfers between devices, shards(): send = lax.ppermute(attend(True, qkv, out_weight), 'col', CORES)  8.26 us
    ppermute x1, starting transfers between devices, shards(): rest = lax.ppermute(half, 'col', CORES)  3.41 us
  transfers between devices with their start and end apart: 2, of which 2 were waited for; matrix products, arithmetic and copies ran while one was open for 0% of the time, Pallas kernels for 1%

profile of v4, /device:TPU:1, one launch (start us, length us, event | category | flops | bytes accessed | tf_op | source)
XLA Modules:
  0.0 87.6 jit_solution(17613572623856451208)
XLA Ops:
  0.0 0.0 copy-start
  0.0 0.0 copy-start.2
  0.0 1.0 %copy-done.2 = bf16[384,384]{1,0:T(8,128)(2,1)S(1)} copy-done((bf16[384,384]{1,0:T(8,128)(2,1)S(1)}, bf16[384,384]{1,0:T(8,128)(2,1)}, u32[]{:S(2)}) %copy-start.2) | copy-done | bytes 294936
  1.0 0.3 center.1
  1.3 0.0 copy-start.1
  1.3 0.0 copy-done
  1.4 0.7 copy-done.1
  2.0 0.9 %partial.1 = bf16[4,880,128]{2,1,0:T(8,128)(2,1)S(1)} custom-call(f32[384,384]{1,0:T(8,128)S(1)} %get-tuple-element.7.x_ref, f32[4,8,128]{2,1,0:T(8,128)S(1)} %get-tuple-element.8.s_ref, f32[384]{0:T(512)S(1)} %copy-done.1, bf16[3,384,384]{2,1,0:T(8,128)(2,1)S(1)} %bitcast.5), custom_call_target="tpu_custom_call" | custom-call | tf_op jit(solution)/shard_map/partial/pallas_call | solution.py:273
  3.0 13.0 %all_to_all.25.refs_0_ = bf16[4,880,128]{2,1,0:T(8,128)(2,1)S(1)} all-to-all(bf16[4,880,128]{2,1,0:T(8,128)(2,1)S(1)} %partial.1), channel_id=1, replica_groups={{0,32,256,288},{64,96,320,352},{128,160,384,416},{192,224,448,480},{1,3..., dimensions={0} | all-to-all | bytes 1802240 | tf_op jit(solution)/shard_map/all_to_all | solution.py:244
  16.0 0.4 merge.1
  16.4 20.8 %all_to_all.26.refs_0_ = bf16[4,232,128]{2,1,0:T(8,128)(2,1)S(1)} all-to-all(bf16[4,232,128]{2,1,0:T(8,128)(2,1)S(1)} %merge.1), channel_id=1, replica_groups={{0,64,128,192},{32,96,160,224},{256,320,384,448},{288,352,416,480},{1,6..., dimensions={0} | all-to-all | bytes 475136 | tf_op jit(solution)/shard_map/all_to_all | solution.py:244
  37.2 0.2 norm.1
  37.5 10.6 %all_to_all.27 = bf16[4,24,1152]{2,1,0:T(8,128)(2,1)S(1)} all-to-all(bf16[4,24,1152]{2,1,0:T(8,128)(2,1)S(1)} %broadcast_in_dim.8), channel_id=1, replica_groups={{0,64,128,192},{32,96,160,224},{256,320,384,448},{288,352,416,480},{1,6..., dimensions={0} | all-to-all | bytes 442368 | tf_op jit(solution)/shard_map/all_to_all | solution.py:244
  48.1 0.1 broadcast_in_dim.10
  48.1 0.0 copy-start.3
  48.2 10.5 %all_to_all.28 = bf16[4,96,1152]{2,1,0:T(8,128)(2,1)S(1)} all-to-all(bf16[4,96,1152]{2,1,0:T(8,128)(2,1)S(1)} %broadcast_in_dim.10), channel_id=1, replica_groups={{0,32,256,288},{64,96,320,352},{128,160,384,416},{192,224,448,480},{1,3..., dimensions={0} | all-to-all | bytes 1769472 | tf_op jit(solution)/shard_map/all_to_all | solution.py:244
  58.7 0.0 copy-done.3
  58.7 0.8 attend.3
  59.5 8.3 %collective-permute-start = (bf16[192,384]{1,0:T(8,128)(2,1)S(1)}, bf16[192,384]{1,0:T(8,128)(2,1)S(1)}, u32[]{:S(2)}, u32[]{:S(2)}) collective-permute-start(bf16[192,384]{1,0:T(8,128)(2,1)S(1)} %attend.3), channel_id=1, source_target_pairs={{0,4},{4,0},{8,12},{12,8},{16,20},{20,16},{24,28},{28,24},{1,5},{5... | collective-permute-start | bytes 442376 | tf_op jit(solution)/shard_map/ppermute | solution.py:295
  67.8 0.8 attend.2
  68.6 0.1 collective-permute-done
  68.8 0.1 broadcast_in_dim.22
  68.9 13.5 %all_to_all.29 = bf16[4,192,384]{2,1,0:T(8,128)(2,1)S(1)} all-to-all(bf16[4,192,384]{2,1,0:T(8,128)(2,1)S(1)} %broadcast_in_dim.22), channel_id=1, replica_groups={{0,8,16,24},{4,12,20,28},{1,9,17,25},{5,13,21,29},{2,10,18,26},{6,14,22..., dimensions={0} | all-to-all | bytes 1179648 | tf_op jit(solution)/shard_map/all_to_all | solution.py:244
  82.3 0.1 reduce_sum.12
  82.4 3.4 %collective-permute-start.1 = (bf16[192,384]{1,0:T(8,128)(2,1)S(1)}, bf16[192,384]{1,0:T(8,128)(2,1)S(1)}, u32[]{:S(2)}, u32[]{:S(2)}) collective-permute-start(bf16[192,384]{1,0:T(8,128)(2,1)S(1)} %reduce_sum.12), channel_id=1, source_target_pairs={{0,4},{4,0},{8,12},{12,8},{16,20},{20,16},{24,28},{28,24},{1,5},{5... | collective-permute-start | bytes 442376 | tf_op jit(solution)/shard_map/ppermute | solution.py:299
  85.9 1.0 %collective-permute-done.1 = bf16[192,384]{1,0:T(8,128)(2,1)S(1)} collective-permute-done((bf16[192,384]{1,0:T(8,128)(2,1)S(1)}, bf16[192,384]{1,0:T(8,128)(2,1)S(1)}, u32[]{:S(2)}, u32[]{:S(2)}) %collective-permute-start.1) | collective-permute-done | bytes 147488 | tf_op jit(solution)/shard_map/ppermute | solution.py:299
  86.9 0.7 pad_maximum_fusion
  (3 shorter events, 0.1 us)
Async XLA Ops:
  0.0 1.3 %copy-start = (bf16[384,3,384]{2,0,1:T(8,128)(2,1)S(1)}, bf16[384,3,384]{2,0,1:T(8,128)(2,1)}, u32[]{:S(2)}) copy-start(bf16[384,3,384]{2,0,1:T(8,128)(2,1)} %param.6) | copy-start | bytes 2654212
  0.0 1.0 %copy-start.2 = (bf16[384,384]{1,0:T(8,128)(2,1)S(1)}, bf16[384,384]{1,0:T(8,128)(2,1)}, u32[]{:S(2)}) copy-start(bf16[384,384]{1,0:T(8,128)(2,1)} %x_ref.1) | copy-start | bytes 884740
  1.3 0.7 copy-start.1
  48.1 10.6 %copy-start.3 = (bf16[384,384]{1,0:T(8,128)(2,1)S(1)}, bf16[384,384]{1,0:T(8,128)(2,1)}, u32[]{:S(2)}) copy-start(bf16[384,384]{1,0:T(8,128)(2,1)} %refs_1_.3) | copy-start | bytes 884740
  59.5 9.3 %collective-permute-start = (bf16[192,384]{1,0:T(8,128)(2,1)S(1)}, bf16[192,384]{1,0:T(8,128)(2,1)S(1)}, u32[]{:S(2)}, u32[]{:S(2)}) collective-permute-start(bf16[192,384]{1,0:T(8,128)(2,1)S(1)} %attend.3), channel_id=1, source_target_pairs={{0,4},{4,0},{8,12},{12,8},{16,20},{20,16},{24,28},{28,24},{1,5},{5... | collective-permute-start | bytes 442376 | tf_op jit(solution)/shard_map/ppermute | solution.py:295
  82.4 4.4 %collective-permute-start.1 = (bf16[192,384]{1,0:T(8,128)(2,1)S(1)}, bf16[192,384]{1,0:T(8,128)(2,1)S(1)}, u32[]{:S(2)}, u32[]{:S(2)}) collective-permute-start(bf16[192,384]{1,0:T(8,128)(2,1)S(1)} %reduce_sum.12), channel_id=1, source_target_pairs={{0,4},{4,0},{8,12},{12,8},{16,20},{20,16},{24,28},{28,24},{1,5},{5... | collective-permute-start | bytes 442376 | tf_op jit(solution)/shard_map/ppermute | solution.py:299

commit v5 on v4

--- a/solution.py
+++ b/solution.py
@@ -17,8 +17,9 @@
 LIMIT = pltpu.CompilerParams(vmem_limit_bytes=20 * 2**20)
 
 CLASSES = 4
-NEAR = [[8 * y + 2 * i + b for y in range(2) for b in range(2)] for i in range(4)]
-FAR = [[8 * y + 2 * i + b for i in range(4)] for y in range(2) for b in range(2)]
+PLACES = ((1, 2, 4, 7), (0, 3, 5, 6))
+NEAR = [[8 * y + place[i] for y in range(2) for place in PLACES] for i in range(4)]
+FAR = [[8 * y + z for z in place] for y in range(2) for place in PLACES]
 CORES = [(c, c ^ 1) for c in range(8)]
 CHIPS = [[0, 2, 4, 6], [1, 3, 5, 7]]
 

time: 88 us -> 86.5 us (0.983)
  starting transfers between devices: 11.7 us -> 10.6 us
  blocking collectives: 68.5 us -> 67.5 us
    ppermute x1, starting transfers between devices: 8.26 us -> 7.21 us  [shards(): send = lax.ppermute(attend(True, qkv, out_weight), 'col', CORES)]
    all_to_all x5, blocking collectives: 68.5 us -> 67.5 us  [exchange(): return lax.all_to_all(a, axis, 0, 0, tiled=True, axis_index_groups=groups)]
where the time goes in v5:
time: 86.5 us; the launch traced here: 85.6 us
  blocking collectives  67.5 us (78%)
  starting transfers between devices  10.6 us (12%)
  Pallas kernels  3.48 us (4%)
  local copies, waits for them, and re-layouts  1.85 us (2%)
  waiting for transfers between devices  1.13 us (1%)
  other arithmetic  0.91 us (1%)
    all_to_all x5, blocking collectives, exchange(): return lax.all_to_all(a, axis, 0, 0, tiled=True, axis_index_groups=groups)  67.5 us
    ppermute x1, starting transfers between devices, shards(): send = lax.ppermute(attend(True, qkv, out_weight), 'col', CORES)  7.21 us
    ppermute x1, starting transfers between devices, shards(): rest = lax.ppermute(half, 'col', CORES)  3.41 us
  transfers between devices with their start and end apart: 2, of which 2 were waited for; matrix products, arithmetic and copies ran while one was open for 0% of the time, Pallas kernels for 1%

profile of v5, /device:TPU:1, one launch (start us, length us, event | category | flops | bytes accessed | tf_op | source)
XLA Modules:
  0.0 85.6 jit_solution(7374428533116382192)
XLA Ops:
  0.0 0.0 copy-start
  0.0 0.0 copy-start.2
  0.0 1.0 %copy-done.2 = bf16[384,384]{1,0:T(8,128)(2,1)S(1)} copy-done((bf16[384,384]{1,0:T(8,128)(2,1)S(1)}, bf16[384,384]{1,0:T(8,128)(2,1)}, u32[]{:S(2)}) %copy-start.2) | copy-done | bytes 294936
  1.0 0.3 center.1
  1.3 0.0 copy-start.1
  1.3 0.0 copy-done
  1.4 0.7 copy-done.1
  2.0 0.9 %partial.1 = bf16[4,880,128]{2,1,0:T(8,128)(2,1)S(1)} custom-call(f32[384,384]{1,0:T(8,128)S(1)} %get-tuple-element.7.x_ref, f32[4,8,128]{2,1,0:T(8,128)S(1)} %get-tuple-element.8.s_ref, f32[384]{0:T(512)S(1)} %copy-done.1, bf16[3,384,384]{2,1,0:T(8,128)(2,1)S(1)} %bitcast.5), custom_call_target="tpu_custom_call" | custom-call | tf_op jit(solution)/shard_map/partial/pallas_call | solution.py:274
  3.0 12.8 %all_to_all.25.refs_0_ = bf16[4,880,128]{2,1,0:T(8,128)(2,1)S(1)} all-to-all(bf16[4,880,128]{2,1,0:T(8,128)(2,1)S(1)} %partial.1), channel_id=1, replica_groups={{32,0,288,256},{64,96,320,352},{128,160,384,416},{224,192,480,448},{33,..., dimensions={0} | all-to-all | bytes 1802240 | tf_op jit(solution)/shard_map/all_to_all | solution.py:245
  15.8 0.4 merge.1
  16.2 20.2 %all_to_all.26.refs_0_ = bf16[4,232,128]{2,1,0:T(8,128)(2,1)S(1)} all-to-all(bf16[4,232,128]{2,1,0:T(8,128)(2,1)S(1)} %merge.1), channel_id=1, replica_groups={{32,64,128,224},{0,96,160,192},{288,320,384,480},{256,352,416,448},{33,..., dimensions={0} | all-to-all | bytes 475136 | tf_op jit(solution)/shard_map/all_to_all | solution.py:245
  36.4 0.2 norm.1
  36.6 10.3 %all_to_all.27 = bf16[4,24,1152]{2,1,0:T(8,128)(2,1)S(1)} all-to-all(bf16[4,24,1152]{2,1,0:T(8,128)(2,1)S(1)} %broadcast_in_dim.8), channel_id=1, replica_groups={{32,64,128,224},{0,96,160,192},{288,320,384,480},{256,352,416,448},{33,..., dimensions={0} | all-to-all | bytes 442368 | tf_op jit(solution)/shard_map/all_to_all | solution.py:245
  46.9 0.1 broadcast_in_dim.10
  47.0 0.0 copy-start.3
  47.0 10.8 %all_to_all.28 = bf16[4,96,1152]{2,1,0:T(8,128)(2,1)S(1)} all-to-all(bf16[4,96,1152]{2,1,0:T(8,128)(2,1)S(1)} %broadcast_in_dim.10), channel_id=1, replica_groups={{32,0,288,256},{64,96,320,352},{128,160,384,416},{224,192,480,448},{33,..., dimensions={0} | all-to-all | bytes 1769472 | tf_op jit(solution)/shard_map/all_to_all | solution.py:245
  57.8 0.0 copy-done.3
  57.8 0.8 attend.3
  58.6 7.2 %collective-permute-start = (bf16[192,384]{1,0:T(8,128)(2,1)S(1)}, bf16[192,384]{1,0:T(8,128)(2,1)S(1)}, u32[]{:S(2)}, u32[]{:S(2)}) collective-permute-start(bf16[192,384]{1,0:T(8,128)(2,1)S(1)} %attend.3), channel_id=1, source_target_pairs={{0,4},{4,0},{8,12},{12,8},{16,20},{20,16},{24,28},{28,24},{1,5},{5... | collective-permute-start | bytes 442376 | tf_op jit(solution)/shard_map/ppermute | solution.py:296
  65.8 0.8 attend.2
  66.6 0.2 collective-permute-done
  66.8 0.1 broadcast_in_dim.22
  66.9 13.4 %all_to_all.29 = bf16[4,192,384]{2,1,0:T(8,128)(2,1)S(1)} all-to-all(bf16[4,192,384]{2,1,0:T(8,128)(2,1)S(1)} %broadcast_in_dim.22), channel_id=1, replica_groups={{0,8,16,24},{4,12,20,28},{1,9,17,25},{5,13,21,29},{2,10,18,26},{6,14,22..., dimensions={0} | all-to-all | bytes 1179648 | tf_op jit(solution)/shard_map/all_to_all | solution.py:245
  80.3 0.1 reduce_sum.12
  80.4 3.4 %collective-permute-start.1 = (bf16[192,384]{1,0:T(8,128)(2,1)S(1)}, bf16[192,384]{1,0:T(8,128)(2,1)S(1)}, u32[]{:S(2)}, u32[]{:S(2)}) collective-permute-start(bf16[192,384]{1,0:T(8,128)(2,1)S(1)} %reduce_sum.12), channel_id=1, source_target_pairs={{0,4},{4,0},{8,12},{12,8},{16,20},{20,16},{24,28},{28,24},{1,5},{5... | collective-permute-start | bytes 442376 | tf_op jit(solution)/shard_map/ppermute | solution.py:300
  83.9 1.0 %collective-permute-done.1 = bf16[192,384]{1,0:T(8,128)(2,1)S(1)} collective-permute-done((bf16[192,384]{1,0:T(8,128)(2,1)S(1)}, bf16[192,384]{1,0:T(8,128)(2,1)S(1)}, u32[]{:S(2)}, u32[]{:S(2)}) %collective-permute-start.1) | collective-permute-done | bytes 147488 | tf_op jit(solution)/shard_map/ppermute | solution.py:300
  84.9 0.7 pad_maximum_fusion
  (3 shorter events, 0.1 us)
Async XLA Ops:
  0.0 1.3 %copy-start = (bf16[384,3,384]{2,0,1:T(8,128)(2,1)S(1)}, bf16[384,3,384]{2,0,1:T(8,128)(2,1)}, u32[]{:S(2)}) copy-start(bf16[384,3,384]{2,0,1:T(8,128)(2,1)} %param.6) | copy-start | bytes 2654212
  0.0 1.0 %copy-start.2 = (bf16[384,384]{1,0:T(8,128)(2,1)S(1)}, bf16[384,384]{1,0:T(8,128)(2,1)}, u32[]{:S(2)}) copy-start(bf16[384,384]{1,0:T(8,128)(2,1)} %x_ref.1) | copy-start | bytes 884740
  1.3 0.7 copy-start.1
  47.0 10.8 %copy-start.3 = (bf16[384,384]{1,0:T(8,128)(2,1)S(1)}, bf16[384,384]{1,0:T(8,128)(2,1)}, u32[]{:S(2)}) copy-start(bf16[384,384]{1,0:T(8,128)(2,1)} %refs_1_.3) | copy-start | bytes 884740
  58.6 8.2 %collective-permute-start = (bf16[192,384]{1,0:T(8,128)(2,1)S(1)}, bf16[192,384]{1,0:T(8,128)(2,1)S(1)}, u32[]{:S(2)}, u32[]{:S(2)}) collective-permute-start(bf16[192,384]{1,0:T(8,128)(2,1)S(1)} %attend.3), channel_id=1, source_target_pairs={{0,4},{4,0},{8,12},{12,8},{16,20},{20,16},{24,28},{28,24},{1,5},{5... | collective-permute-start | bytes 442376 | tf_op jit(solution)/shard_map/ppermute | solution.py:296
  80.4 4.4 %collective-permute-start.1 = (bf16[192,384]{1,0:T(8,128)(2,1)S(1)}, bf16[192,384]{1,0:T(8,128)(2,1)S(1)}, u32[]{:S(2)}, u32[]{:S(2)}) collective-permute-start(bf16[192,384]{1,0:T(8,128)(2,1)S(1)} %reduce_sum.12), channel_id=1, source_target_pairs={{0,4},{4,0},{8,12},{12,8},{16,20},{20,16},{24,28},{28,24},{1,5},{5... | collective-permute-start | bytes 442376 | tf_op jit(solution)/shard_map/ppermute | solution.py:300

commit v6 on v5

--- a/solution.py
+++ b/solution.py
@@ -17,7 +17,7 @@
 LIMIT = pltpu.CompilerParams(vmem_limit_bytes=20 * 2**20)
 
 CLASSES = 4
-PLACES = ((1, 2, 4, 7), (0, 3, 5, 6))
+PLACES = ((1, 3, 4, 6), (0, 2, 5, 7))
 NEAR = [[8 * y + place[i] for y in range(2) for place in PLACES] for i in range(4)]
 FAR = [[8 * y + z for z in place] for y in range(2) for place in PLACES]
 CORES = [(c, c ^ 1) for c in range(8)]
@@ -117,15 +117,15 @@
     size = tokens // CLASSES
     columns = w_ref.shape[2]
     gain = g_ref[...].reshape(1, width)
-    scaled = (x_ref[...] * gain).astype(jnp.bfloat16)
     high = rounded(gain)
     line = lax.broadcasted_iota(jnp.int32, (16, width), 0)
     gains = jnp.where(line == 0, high, jnp.where(line == 1, gain - high, 0.0)).astype(jnp.bfloat16)
+    scaled = jnp.concatenate([(x_ref[...] * gain).astype(jnp.bfloat16), gains], axis=0)
     sums = []
     for part in range(3):
-        weight = w_ref[part]
-        product = dot32(scaled, weight).astype(jnp.bfloat16)
-        c = jnp.sum(dot32(gains, weight), axis=0, keepdims=True)
+        both = dot32(scaled, w_ref[part])
+        product = both[:tokens].astype(jnp.bfloat16)
+        c = jnp.sum(both[tokens:], axis=0, keepdims=True)
         for at in range(0, columns, LANES):
             to = len(sums) * size
             for block in range(CLASSES):

time: 86.5 us -> 85.7 us (level)
  no operation moved by 1% of the time
where the time goes in v6:
time: 85.7 us; the launch traced here: 85.3 us
  blocking collectives  67.1 us (78%)
  starting transfers between devices  10.8 us (13%)
  Pallas kernels  3.41 us (4%)
  local copies, waits for them, and re-layouts  1.85 us (2%)
  waiting for transfers between devices  1.13 us (1%)
  other arithmetic  0.91 us (1%)
    all_to_all x5, blocking collectives, exchange(): return lax.all_to_all(a, axis, 0, 0, tiled=True, axis_index_groups=groups)  67.1 us
    ppermute x1, starting transfers between devices, shards(): send = lax.ppermute(attend(True, qkv, out_weight), 'col', CORES)  7.36 us
    ppermute x1, starting transfers between devices, shards(): rest = lax.ppermute(half, 'col', CORES)  3.41 us
    unnamed x8, local copies, waits for them, and re-layouts  1.72 us
  transfers between devices with their start and end apart: 2, of which 2 were waited for; matrix products, arithmetic and copies ran while one was open for 0% of the time, Pallas kernels for 1%

profile of v6, /device:TPU:1, one launch (start us, length us, event | category | flops | bytes accessed | tf_op | source)
XLA Modules:
  0.0 85.3 jit_solution(1529399945723016194)
XLA Ops:
  0.0 0.0 copy-start
  0.0 0.0 copy-start.2
  0.0 1.0 %copy-done.2 = bf16[384,384]{1,0:T(8,128)(2,1)S(1)} copy-done((bf16[384,384]{1,0:T(8,128)(2,1)S(1)}, bf16[384,384]{1,0:T(8,128)(2,1)}, u32[]{:S(2)}) %copy-start.2) | copy-done | bytes 294936
  1.0 0.3 center.1
  1.3 0.0 copy-start.1
  1.3 0.0 copy-done
  1.4 0.7 copy-done.1
  2.0 0.9 %partial.1 = bf16[4,880,128]{2,1,0:T(8,128)(2,1)S(1)} custom-call(f32[384,384]{1,0:T(8,128)S(1)} %get-tuple-element.7.x_ref, f32[4,8,128]{2,1,0:T(8,128)S(1)} %get-tuple-element.8.s_ref, f32[384]{0:T(512)S(1)} %copy-done.1, bf16[3,384,384]{2,1,0:T(8,128)(2,1)S(1)} %bitcast.5), custom_call_target="tpu_custom_call" | custom-call | tf_op jit(solution)/shard_map/partial/pallas_call | solution.py:274
  2.9 12.8 %all_to_all.25.refs_0_ = bf16[4,880,128]{2,1,0:T(8,128)(2,1)S(1)} all-to-all(bf16[4,880,128]{2,1,0:T(8,128)(2,1)S(1)} %partial.1), channel_id=1, replica_groups={{32,0,288,256},{96,64,352,320},{128,160,384,416},{192,224,448,480},{33,..., dimensions={0} | all-to-all | bytes 1802240 | tf_op jit(solution)/shard_map/all_to_all | solution.py:245
  15.7 0.4 merge.1
  16.1 19.3 %all_to_all.26.refs_0_ = bf16[4,232,128]{2,1,0:T(8,128)(2,1)S(1)} all-to-all(bf16[4,232,128]{2,1,0:T(8,128)(2,1)S(1)} %merge.1), channel_id=1, replica_groups={{32,96,128,192},{0,64,160,224},{288,352,384,448},{256,320,416,480},{33,..., dimensions={0} | all-to-all | bytes 475136 | tf_op jit(solution)/shard_map/all_to_all | solution.py:245
  35.5 0.2 norm.1
  35.7 9.9 %all_to_all.27 = bf16[4,24,1152]{2,1,0:T(8,128)(2,1)S(1)} all-to-all(bf16[4,24,1152]{2,1,0:T(8,128)(2,1)S(1)} %broadcast_in_dim.8), channel_id=1, replica_groups={{32,96,128,192},{0,64,160,224},{288,352,384,448},{256,320,416,480},{33,..., dimensions={0} | all-to-all | bytes 442368 | tf_op jit(solution)/shard_map/all_to_all | solution.py:245
  45.6 0.1 broadcast_in_dim.10
  45.6 0.0 copy-start.3
  45.6 11.6 %all_to_all.28 = bf16[4,96,1152]{2,1,0:T(8,128)(2,1)S(1)} all-to-all(bf16[4,96,1152]{2,1,0:T(8,128)(2,1)S(1)} %broadcast_in_dim.10), channel_id=1, replica_groups={{32,0,288,256},{96,64,352,320},{128,160,384,416},{192,224,448,480},{33,..., dimensions={0} | all-to-all | bytes 1769472 | tf_op jit(solution)/shard_map/all_to_all | solution.py:245
  57.3 0.0 copy-done.3
  57.3 0.8 attend.3
  58.1 7.4 %collective-permute-start = (bf16[192,384]{1,0:T(8,128)(2,1)S(1)}, bf16[192,384]{1,0:T(8,128)(2,1)S(1)}, u32[]{:S(2)}, u32[]{:S(2)}) collective-permute-start(bf16[192,384]{1,0:T(8,128)(2,1)S(1)} %attend.3), channel_id=1, source_target_pairs={{0,4},{4,0},{8,12},{12,8},{16,20},{20,16},{24,28},{28,24},{1,5},{5... | collective-permute-start | bytes 442376 | tf_op jit(solution)/shard_map/ppermute | solution.py:296
  65.5 0.8 attend.2
  66.3 0.1 collective-permute-done
  66.5 0.1 broadcast_in_dim.22
  66.5 13.5 %all_to_all.29 = bf16[4,192,384]{2,1,0:T(8,128)(2,1)S(1)} all-to-all(bf16[4,192,384]{2,1,0:T(8,128)(2,1)S(1)} %broadcast_in_dim.22), channel_id=1, replica_groups={{0,8,16,24},{4,12,20,28},{1,9,17,25},{5,13,21,29},{2,10,18,26},{6,14,22..., dimensions={0} | all-to-all | bytes 1179648 | tf_op jit(solution)/shard_map/all_to_all | solution.py:245
  80.0 0.1 reduce_sum.12
  80.1 3.4 %collective-permute-start.1 = (bf16[192,384]{1,0:T(8,128)(2,1)S(1)}, bf16[192,384]{1,0:T(8,128)(2,1)S(1)}, u32[]{:S(2)}, u32[]{:S(2)}) collective-permute-start(bf16[192,384]{1,0:T(8,128)(2,1)S(1)} %reduce_sum.12), channel_id=1, source_target_pairs={{0,4},{4,0},{8,12},{12,8},{16,20},{20,16},{24,28},{28,24},{1,5},{5... | collective-permute-start | bytes 442376 | tf_op jit(solution)/shard_map/ppermute | solution.py:300
  83.5 1.0 %collective-permute-done.1 = bf16[192,384]{1,0:T(8,128)(2,1)S(1)} collective-permute-done((bf16[192,384]{1,0:T(8,128)(2,1)S(1)}, bf16[192,384]{1,0:T(8,128)(2,1)S(1)}, u32[]{:S(2)}, u32[]{:S(2)}) %collective-permute-start.1) | collective-permute-done | bytes 147488 | tf_op jit(solution)/shard_map/ppermute | solution.py:300
  84.5 0.7 pad_maximum_fusion
  (3 shorter events, 0.1 us)
Async XLA Ops:
  0.0 1.3 %copy-start = (bf16[384,3,384]{2,0,1:T(8,128)(2,1)S(1)}, bf16[384,3,384]{2,0,1:T(8,128)(2,1)}, u32[]{:S(2)}) copy-start(bf16[384,3,384]{2,0,1:T(8,128)(2,1)} %param.6) | copy-start | bytes 2654212
  0.0 1.0 %copy-start.2 = (bf16[384,384]{1,0:T(8,128)(2,1)S(1)}, bf16[384,384]{1,0:T(8,128)(2,1)}, u32[]{:S(2)}) copy-start(bf16[384,384]{1,0:T(8,128)(2,1)} %x_ref.1) | copy-start | bytes 884740
  1.3 0.7 copy-start.1
  45.6 11.6 %copy-start.3 = (bf16[384,384]{1,0:T(8,128)(2,1)S(1)}, bf16[384,384]{1,0:T(8,128)(2,1)}, u32[]{:S(2)}) copy-start(bf16[384,384]{1,0:T(8,128)(2,1)} %refs_1_.3) | copy-start | bytes 884740
  58.1 8.4 %collective-permute-start = (bf16[192,384]{1,0:T(8,128)(2,1)S(1)}, bf16[192,384]{1,0:T(8,128)(2,1)S(1)}, u32[]{:S(2)}, u32[]{:S(2)}) collective-permute-start(bf16[192,384]{1,0:T(8,128)(2,1)S(1)} %attend.3), channel_id=1, source_target_pairs={{0,4},{4,0},{8,12},{12,8},{16,20},{20,16},{24,28},{28,24},{1,5},{5... | collective-permute-start | bytes 442376 | tf_op jit(solution)/shard_map/ppermute | solution.py:296
  80.1 4.4 %collective-permute-start.1 = (bf16[192,384]{1,0:T(8,128)(2,1)S(1)}, bf16[192,384]{1,0:T(8,128)(2,1)S(1)}, u32[]{:S(2)}, u32[]{:S(2)}) collective-permute-start(bf16[192,384]{1,0:T(8,128)(2,1)S(1)} %reduce_sum.12), channel_id=1, source_target_pairs={{0,4},{4,0},{8,12},{12,8},{16,20},{20,16},{24,28},{28,24},{1,5},{5... | collective-permute-start | bytes 442376 | tf_op jit(solution)/shard_map/ppermute | solution.py:300

commit v7 on v6

--- a/solution.py
+++ b/solution.py
@@ -211,11 +211,14 @@
     largest = jnp.max(scores, axis=1, keepdims=True)
     exponent = jnp.exp((scores - largest) * scaling)
     inverse = 1.0 / jnp.sum(exponent, axis=1, keepdims=True)
-    shares = (exponent * inverse).astype(jnp.bfloat16)
+    shares = exponent.astype(jnp.bfloat16)
     outs = [
-        dot32(
-            shares[head * half : (head + 1) * half],
-            x_ref[:, 2 * columns + at : 2 * columns + at + K],
+        (
+            dot32(
+                shares[head * half : (head + 1) * half],
+                x_ref[:, 2 * columns + at : 2 * columns + at + K],
+            )
+            * inverse[head * half : (head + 1) * half]
         ).astype(jnp.bfloat16)
         for head, at in enumerate(starts)
     ]
@@ -235,6 +238,21 @@
             flops=4 * flops, bytes_accessed=2 * count * wide, transcendentals=0
         ),
     )(qkv, weight)
+
+
+def write_kernel(own_ref, rest_ref, o_ref, sems):
+    half = own_ref.shape[0]
+    core = lax.rem(lax.axis_index("col"), 2)
+    copies = [
+        pltpu.make_async_copy(
+            ref, o_ref.at[pl.ds(pl.multiple_of(at * half, half), half), :], sems.at[slot]
+        )
+        for slot, (ref, at) in enumerate(((own_ref, core), (rest_ref, 1 - core)))
+    ]
+    for copy in copies:
+        copy.start()
+    for copy in copies:
+        copy.wait()
 
 
 def added(a, b):
@@ -298,10 +316,14 @@
     terms = spread(pair, "col", CHIPS)
     half = jnp.sum(terms.astype(jnp.float32), axis=0).astype(jnp.bfloat16)
     rest = lax.ppermute(half, "col", CORES)
-    core = lax.rem(lax.axis_index("col"), 2)
-    return jnp.concatenate(
-        [jnp.where(core == 0, half, rest), jnp.where(core == 0, rest, half)], axis=0
-    )
+    return pl.pallas_call(
+        write_kernel,
+        out_shape=like((count, width)),
+        out_specs=pl.BlockSpec(memory_space=pl.ANY),
+        scratch_shapes=[pltpu.SemaphoreType.DMA((2,))],
+        name="write",
+        compiler_params=LIMIT,
+    )(half, rest)
 
 
 def solution(mesh):

time: 85.7 us -> 85.5 us (level)
  no operation moved by 1% of the time
where the time goes in v7:
time: 85.5 us; the launch traced here: 85.1 us
  blocking collectives  67.1 us (78%)
  starting transfers between devices  10.8 us (13%)
  Pallas kernels  3.95 us (5%)
  local copies, waits for them, and re-layouts  1.85 us (2%)
  waiting for transfers between devices  1.23 us (1%)
    all_to_all x5, blocking collectives, exchange(): return lax.all_to_all(a, axis, 0, 0, tiled=True, axis_index_groups=groups)  67.1 us
    ppermute x1, starting transfers between devices, shards(): send = lax.ppermute(attend(True, qkv, out_weight), 'col', CORES)  7.36 us
    ppermute x1, starting transfers between devices, shards(): rest = lax.ppermute(half, 'col', CORES)  3.41 us
    unnamed x8, local copies, waits for them, and re-layouts  1.72 us
  transfers between devices with their start and end apart: 2, of which 2 were waited for; matrix products, arithmetic and copies ran while one was open for 0% of the time, Pallas kernels for 1%

profile of v7, /device:TPU:1, one launch (start us, length us, event | category | flops | bytes accessed | tf_op | source)
XLA Modules:
  0.0 85.1 jit_solution(8369720653246006584)
XLA Ops:
  0.0 0.0 copy-start
  0.0 0.0 copy-start.2
  0.0 1.0 %copy-done.2 = bf16[384,384]{1,0:T(8,128)(2,1)S(1)} copy-done((bf16[384,384]{1,0:T(8,128)(2,1)S(1)}, bf16[384,384]{1,0:T(8,128)(2,1)}, u32[]{:S(2)}) %copy-start.2) | copy-done | bytes 294936
  1.0 0.3 center.1
  1.3 0.0 copy-start.1
  1.3 0.0 copy-done
  1.4 0.7 copy-done.1
  2.0 0.9 %partial.1 = bf16[4,880,128]{2,1,0:T(8,128)(2,1)S(1)} custom-call(f32[384,384]{1,0:T(8,128)S(1)} %get-tuple-element.7.x_ref, f32[4,8,128]{2,1,0:T(8,128)S(1)} %get-tuple-element.8.s_ref, f32[384]{0:T(512)S(1)} %copy-done.1, bf16[3,384,384]{2,1,0:T(8,128)(2,1)S(1)} %bitcast.5), custom_call_target="tpu_custom_call" | custom-call | tf_op jit(solution)/shard_map/partial/pallas_call | solution.py:292
  2.9 12.8 %all_to_all.25.refs_0_ = bf16[4,880,128]{2,1,0:T(8,128)(2,1)S(1)} all-to-all(bf16[4,880,128]{2,1,0:T(8,128)(2,1)S(1)} %partial.1), channel_id=1, replica_groups={{32,0,288,256},{96,64,352,320},{128,160,384,416},{192,224,448,480},{33,..., dimensions={0} | all-to-all | bytes 1802240 | tf_op jit(solution)/shard_map/all_to_all | solution.py:263
  15.7 0.4 merge.1
  16.1 19.3 %all_to_all.26.refs_0_ = bf16[4,232,128]{2,1,0:T(8,128)(2,1)S(1)} all-to-all(bf16[4,232,128]{2,1,0:T(8,128)(2,1)S(1)} %merge.1), channel_id=1, replica_groups={{32,96,128,192},{0,64,160,224},{288,352,384,448},{256,320,416,480},{33,..., dimensions={0} | all-to-all | bytes 475136 | tf_op jit(solution)/shard_map/all_to_all | solution.py:263
  35.5 0.2 norm.1
  35.7 9.9 %all_to_all.27 = bf16[4,24,1152]{2,1,0:T(8,128)(2,1)S(1)} all-to-all(bf16[4,24,1152]{2,1,0:T(8,128)(2,1)S(1)} %broadcast_in_dim.8), channel_id=1, replica_groups={{32,96,128,192},{0,64,160,224},{288,352,384,448},{256,320,416,480},{33,..., dimensions={0} | all-to-all | bytes 442368 | tf_op jit(solution)/shard_map/all_to_all | solution.py:263
  45.6 0.1 broadcast_in_dim.10
  45.6 0.0 copy-start.3
  45.6 11.6 %all_to_all.28 = bf16[4,96,1152]{2,1,0:T(8,128)(2,1)S(1)} all-to-all(bf16[4,96,1152]{2,1,0:T(8,128)(2,1)S(1)} %broadcast_in_dim.10), channel_id=1, replica_groups={{32,0,288,256},{96,64,352,320},{128,160,384,416},{192,224,448,480},{33,..., dimensions={0} | all-to-all | bytes 1769472 | tf_op jit(solution)/shard_map/all_to_all | solution.py:263
  57.3 0.0 copy-done.3
  57.3 0.7 attend.3
  58.0 7.4 %collective-permute-start = (bf16[192,384]{1,0:T(8,128)(2,1)S(1)}, bf16[192,384]{1,0:T(8,128)(2,1)S(1)}, u32[]{:S(2)}, u32[]{:S(2)}) collective-permute-start(bf16[192,384]{1,0:T(8,128)(2,1)S(1)} %attend.3), channel_id=1, source_target_pairs={{0,4},{4,0},{8,12},{12,8},{16,20},{20,16},{24,28},{28,24},{1,5},{5... | collective-permute-start | bytes 442376 | tf_op jit(solution)/shard_map/ppermute | solution.py:314
  65.4 0.7 attend.2
  66.1 0.2 collective-permute-done
  66.4 0.1 broadcast_in_dim.22
  66.5 13.4 %all_to_all.29 = bf16[4,192,384]{2,1,0:T(8,128)(2,1)S(1)} all-to-all(bf16[4,192,384]{2,1,0:T(8,128)(2,1)S(1)} %broadcast_in_dim.22), channel_id=1, replica_groups={{0,8,16,24},{4,12,20,28},{1,9,17,25},{5,13,21,29},{2,10,18,26},{6,14,22..., dimensions={0} | all-to-all | bytes 1179648 | tf_op jit(solution)/shard_map/all_to_all | solution.py:263
  79.9 0.1 reduce_sum.12.own_ref
  80.0 3.4 %collective-permute-start.1 = (bf16[192,384]{1,0:T(8,128)(2,1)S(1)}, bf16[192,384]{1,0:T(8,128)(2,1)S(1)}, u32[]{:S(2)}, u32[]{:S(2)}) collective-permute-start(bf16[192,384]{1,0:T(8,128)(2,1)S(1)} %reduce_sum.12.own_ref), channel_id=1, source_target_pairs={{0,4},{4,0},{8,12},{12,8},{16,20},{20,16},{24,28},{28,24},{1,5},{5... | collective-permute-start | bytes 442376 | tf_op jit(solution)/shard_map/ppermute | solution.py:318
  83.4 1.0 %collective-permute-done.1.rest_ref = bf16[192,384]{1,0:T(8,128)(2,1)S(1)} collective-permute-done((bf16[192,384]{1,0:T(8,128)(2,1)S(1)}, bf16[192,384]{1,0:T(8,128)(2,1)S(1)}, u32[]{:S(2)}, u32[]{:S(2)}) %collective-permute-start.1) | collective-permute-done | bytes 147488 | tf_op jit(solution)/shard_map/ppermute | solution.py:318
  84.4 0.7 write.1
  (2 shorter events, 0.1 us)
Async XLA Ops:
  0.0 1.3 %copy-start = (bf16[384,3,384]{2,0,1:T(8,128)(2,1)S(1)}, bf16[384,3,384]{2,0,1:T(8,128)(2,1)}, u32[]{:S(2)}) copy-start(bf16[384,3,384]{2,0,1:T(8,128)(2,1)} %param.6) | copy-start | bytes 2654212
  0.0 1.0 %copy-start.2 = (bf16[384,384]{1,0:T(8,128)(2,1)S(1)}, bf16[384,384]{1,0:T(8,128)(2,1)}, u32[]{:S(2)}) copy-start(bf16[384,384]{1,0:T(8,128)(2,1)} %x_ref.1) | copy-start | bytes 884740
  1.3 0.7 copy-start.1
  45.6 11.6 %copy-start.3 = (bf16[384,384]{1,0:T(8,128)(2,1)S(1)}, bf16[384,384]{1,0:T(8,128)(2,1)}, u32[]{:S(2)}) copy-start(bf16[384,384]{1,0:T(8,128)(2,1)} %refs_1_.3) | copy-start | bytes 884740
  58.0 8.4 %collective-permute-start = (bf16[192,384]{1,0:T(8,128)(2,1)S(1)}, bf16[192,384]{1,0:T(8,128)(2,1)S(1)}, u32[]{:S(2)}, u32[]{:S(2)}) collective-permute-start(bf16[192,384]{1,0:T(8,128)(2,1)S(1)} %attend.3), channel_id=1, source_target_pairs={{0,4},{4,0},{8,12},{12,8},{16,20},{20,16},{24,28},{28,24},{1,5},{5... | collective-permute-start | bytes 442376 | tf_op jit(solution)/shard_map/ppermute | solution.py:314
  80.0 4.4 %collective-permute-start.1 = (bf16[192,384]{1,0:T(8,128)(2,1)S(1)}, bf16[192,384]{1,0:T(8,128)(2,1)S(1)}, u32[]{:S(2)}, u32[]{:S(2)}) collective-permute-start(bf16[192,384]{1,0:T(8,128)(2,1)S(1)} %reduce_sum.12.own_ref), channel_id=1, source_target_pairs={{0,4},{4,0},{8,12},{12,8},{16,20},{20,16},{24,28},{28,24},{1,5},{5... | collective-permute-start | bytes 442376 | tf_op jit(solution)/shard_map/ppermute | solution.py:318
